TPU v7x, 512 devices: a whole 4x4x16 slice. The times are simulated.
512 devices in a mesh: gx: 4 (over z_hi), gy: 8 (over y, core), gz: 16 (over x, z_lo).
Axes of the slice: x: 4, y: 4, z: 16 (z_hi: 4, z_lo: 4; z = z_hi * 4 + z_lo), core: 2. Of those that a mesh axis runs over, the one named last changes fastest.
Arguments:
- right_side: float32 [4, 8, 16, 6, 1024], P('gx', 'gy', 'gz'), may hold values from -18 to 18
- grain_diag: float32 [4, 8, 16, 6, 1024], P('gx', 'gy', 'gz'), may hold values from 0.05 to 0.5
- stiffness: float32 [4, 4], replicated, may hold values from 0.3 to 3
- contact_own: int32 [4, 8, 16, 3072], P('gx', 'gy', 'gz'), may hold values from 0 to 1023, as said below
- contact_slot: int32 [4, 8, 16, 3072], P('gx', 'gy', 'gz'), may hold values from 0 to 7679, as said below
- contact_type: int32 [4, 8, 16, 3072], P('gx', 'gy', 'gz'), may hold values from 0 to 4, as said below
- contact_normal: float32 [4, 8, 16, 3, 3072], P('gx', 'gy', 'gz'), may hold values from -1 to 1, as said below
- contact_radii: float32 [4, 8, 16, 2, 3072], P('gx', 'gy', 'gz'), may hold values from 0.4 to 1
Outputs:
- solution_field: float32 [4, 8, 16, 6, 1024], P('gx', 'gy', 'gz')
- residual: float32 [4, 8, 16, 6, 1024], P('gx', 'gy', 'gz')
Inputs may be any that keep to these rules, and one draw needn't show every extreme that they name: `contact_normal`: each normal has unit length. `contact_own`: in the first 2240 slots of a block the own grain differs from the partner; in the last 832 slots the own grain is one of the block's first 256 grains. `contact_slot`: the first 2240 slots of a block hold values below 1024; the slots 3072 - 832 + k * 32 to 2240 + (k + 1) * 32 - 1, for k = 0 to 25, hold values from 1024 + k * 256 to 1024 + (k + 1) * 256 - 1. `contact_type`: the value 4 marks an empty slot.
All inputs are finite; a program needn't handle non-finite values.
Results may differ from a plain program's by a relative error of at most 0.00018.
Values sent between devices are 32-bit elements; how exact they have to be, the bound alone decides.
A program may use at most 64 MiB of HBM per device.

v0:
```python
import jax
import jax.numpy as jnp
import numpy as np
from jax import lax
from jax.sharding import Mesh
from jax.sharding import PartitionSpec as P

ITERS = 4
GX_GY_GZ = ("gx", "gy_0", "gy_1", "gz_0", "gz_1")
GY = ("gy_0", "gy_1")
GZ = ("gz_0", "gz_1")


def one_axis_at_a_time(value, axes):
    for axis in axes:
        value = lax.psum(value, axis)
    return value


def with_halo(block, sides, width):
    for axis, dim in sides:
        count = lax.axis_size(axis)
        forward = [(i, i + 1) for i in range(count - 1)]
        forward.append((count - 1, 0))
        backward = [(target, source) for source, target in forward]
        low = lax.ppermute(
            lax.slice_in_dim(block, block.shape[dim] - width, None, axis=dim), axis, forward
        )
        high = lax.ppermute(lax.slice_in_dim(block, 0, width, axis=dim), axis, backward)
        block = jnp.concatenate([low, block, high], axis=dim)
    return block


def cross(left, right):
    return jnp.stack(
        [
            left[1] * right[2] - left[2] * right[1],
            left[2] * right[0] - left[0] * right[2],
            left[0] * right[1] - left[1] * right[0],
        ]
    )


def lookup(stiffness, ctype):
    total = jnp.zeros((4,) + ctype.shape, stiffness.dtype)
    for which in range(stiffness.shape[1]):
        total = total + stiffness[:, which : which + 1] * (ctype == which)[None].astype(
            stiffness.dtype
        )
    return total


def contact_response(first_u, second_u, normal, radii, coeff):
    normal_k, shear_k, roll_k, twist_k = (coeff[0], coeff[1], coeff[2], coeff[3])
    first_r, second_r = (radii[0], radii[1])
    delta = (
        second_u[:3]
        - second_r * cross(second_u[3:], normal)
        - first_u[:3]
        - first_r * cross(first_u[3:], normal)
    )
    along = jnp.sum(normal * delta, axis=0)
    force = shear_k * delta + (normal_k - shear_k) * along * normal
    theta = second_u[3:] - first_u[3:]
    twist = jnp.sum(normal * theta, axis=0)
    moment = roll_k * theta + (twist_k - roll_k) * twist * normal
    lever = cross(normal, force)
    on_first = jnp.concatenate([force, first_r * lever + moment], axis=0)
    on_second = jnp.concatenate([-force, second_r * lever - moment], axis=0)
    return (on_first, on_second)


def full_position(block):
    return block + (block >= 13).astype(jnp.int32)


def paired(residual, image):
    return (
        one_axis_at_a_time(jnp.sum(residual * residual), GX_GY_GZ),
        one_axis_at_a_time(jnp.sum(residual * image), GX_GY_GZ),
    )


def shards(
    right_side,
    grain_diag,
    stiffness,
    contact_own,
    contact_slot,
    contact_type,
    contact_normal,
    contact_radii,
):
    rhs = right_side[0, 0, 0]
    diag = grain_diag[0, 0, 0]
    grains = rhs.shape[1]
    rim = grains // 4
    owners = contact_own[0, 0, 0]
    slots = contact_slot[0, 0, 0]
    ctype = contact_type[0, 0, 0]
    normal = contact_normal[0, 0, 0]
    radii = contact_radii[0, 0, 0]
    coeff = lookup(stiffness, ctype)
    far_slot = slots >= grains
    rel = jnp.maximum(slots - grains, 0)
    ghost_column = full_position(rel // rim) * rim + rel % rim
    near_grain = jnp.where(far_slot, 0, slots)
    group_size = grains // 32
    remote_count = 26 * group_size
    packed = jnp.stack([owners[-remote_count:], slots[-remote_count:], ctype[-remote_count:]])[
        None, None, None
    ]
    theirs = with_halo(packed, (("gx", 0), (GY, 1), (GZ, 2)), 1).reshape(27, 3, 26, group_size)
    geometry = jnp.concatenate([normal[:, -remote_count:], radii[:, -remote_count:]], axis=0)[
        None, None, None
    ]
    their_geometry = with_halo(geometry, (("gx", 0), (GY, 1), (GZ, 2)), 1).reshape(
        27, 5, 26, group_size
    )
    counts = (lax.axis_size("gx"), lax.axis_size(GY), lax.axis_size(GZ))
    chosen_place = []
    chosen_group = []
    for place in range(27):
        for group in range(26):
            whole = group + (1 if group >= 13 else 0)
            back_x = (place // 9 - 1 + whole // 9 - 1) % counts[0] == 0
            back_y = (place // 3 % 3 - 1 + whole // 3 % 3 - 1) % counts[1] == 0
            back_z = (place % 3 - 1 + whole % 3 - 1) % counts[2] == 0
            if back_x and back_y and back_z:
                chosen_place.append(place)
                chosen_group.append(group)
    place_index = np.array(chosen_place, np.int32)
    group_index = np.array(chosen_group, np.int32)
    picked = theirs[place_index, :, group_index]
    picked_geometry = their_geometry[place_index, :, group_index]
    mirror_coeff = lookup(stiffness, picked[:, 2].reshape(-1))
    mirror_normal = jnp.moveaxis(picked_geometry[:, :3], 1, 0).reshape(3, -1)
    mirror_radii = jnp.moveaxis(picked_geometry[:, 3:], 1, 0).reshape(2, -1)
    mirror_place = jnp.asarray(np.repeat(place_index, group_size))
    mirror_column = mirror_place * rim + picked[:, 0].reshape(-1)
    mirror_mine = ((picked[:, 1] - grains) % rim).reshape(-1)

    def operate(field):
        rims = with_halo(field[None, None, None, :, :rim], (("gx", 0), (GY, 1), (GZ, 2)), 1)
        rim_flat = jnp.moveaxis(rims.reshape(27, 6, rim), 1, 0).reshape(6, 27 * rim)
        first_u = field[:, owners]
        second_u = jnp.where(far_slot[None], rim_flat[:, ghost_column], field[:, near_grain])
        on_first, on_second = contact_response(first_u, second_u, normal, radii, coeff)
        forces = jnp.zeros_like(field).at[:, owners].add(on_first)
        forces = forces.at[:, near_grain].add(jnp.where(far_slot[None], 0.0, on_second))
        their_u = rim_flat[:, mirror_column]
        unused, onto_mine = contact_response(
            their_u, field[:, mirror_mine], mirror_normal, mirror_radii, mirror_coeff
        )
        forces = forces.at[:, mirror_mine].add(onto_mine)
        return diag * field - forces

    solution_field = jnp.zeros_like(rhs)
    residual = rhs
    image = operate(residual)
    norm_now, product = paired(residual, image)
    alpha = norm_now / product
    direction, along = (residual, image)
    for step in range(ITERS):
        solution_field = solution_field + alpha * direction
        residual = residual - alpha * along
        if step + 1 < ITERS:
            image = operate(residual)
            norm_next, product = paired(residual, image)
            ratio = norm_next / norm_now
            alpha = norm_next / (product - ratio * norm_next / alpha)
            direction = residual + ratio * direction
            along = image + ratio * along
            norm_now = norm_next
    return (solution_field[None, None, None], residual[None, None, None])


def solution(mesh):
    torus = Mesh(
        mesh.devices.reshape(mesh.shape["gx"], 4, 2, 4, 4), ("gx", "gy_0", "gy_1", "gz_0", "gz_1")
    )
    placed = (
        P("gx", GY, GZ, None, None),
        P("gx", GY, GZ, None, None),
        P(),
        P("gx", GY, GZ, None),
        P("gx", GY, GZ, None),
        P("gx", GY, GZ, None),
        P("gx", GY, GZ, None, None),
        P("gx", GY, GZ, None, None),
    )
    return jax.shard_map(
        shards,
        mesh=torus,
        in_specs=placed,
        out_specs=(P("gx", GY, GZ, None, None), P("gx", GY, GZ, None, None)),
        check_vma=False,
    )
```

profile of v0, /device:TPU:1, one launch (start us, length us, event | category | flops | bytes accessed | tf_op | source)
XLA Modules:
  0.0 700.7 jit_solution(7459148122912372510)
XLA Ops:
  2.9 13.3 %collective-permute-start.7 = (s32[1,1,1,3,832]{4,3,2,1,0:T(4,128)S(1)}, s32[1,1,1,3,832]{4,3,2,1,0:T(4,128)S(1)}, u32[]{:S(2)}, u32[]{:S(2)}) collective-permute-start(s32[1,1,1,3,832]{4,3,2,1,0:T(4,128)S(1)} %add_bitcast_fusion.1), channel_id=1, source_target_pairs={{128,0},{256,128},{384,256},{0,384},{129,1},{257,129},{385,257},{1... | collective-permute-start | bytes 29960 | tf_op jit(solution)/shard_map/ppermute | solution.py:29
  42.2 8.1 %gather_fusion.2 = f32[3072,6]{1,0:T(8,128)S(1)} fusion(f32[6,1024]{0,1:T(8,128)S(1)} %bitcast.450, s32[3072]{0:T(1024)S(1)} %get-tuple-element.239), kind=kCustom, calls=%fused_computation.2 | custom fusion | bytes 159744 | tf_op jit(solution)/shard_map/gather | solution.py:146
  51.1 8.1 %gather_fusion.1 = f32[3072,6]{1,0:T(8,128)S(1)} fusion(f32[6,1024]{0,1:T(8,128)S(1)} %bitcast.451, s32[3072]{0:T(1024)S(1)} %get-tuple-element.240), kind=kCustom, calls=%fused_computation.1 | custom fusion | bytes 159744 | tf_op jit(solution)/shard_map/gather | solution.py:147
  104.0 10.1 %gather_fusion = f32[3072,6]{1,0:T(8,128)S(1)} fusion(f32[6,6912]{0,1:T(8,128)} %bitcast.453, s32[3072]{0:T(1024)S(1)} %broadcast_clamp_fusion.2), kind=kCustom, calls=%fused_computation | custom fusion | bytes 159744 | tf_op jit(solution)/shard_map/gather | solution.py:147
  117.5 17.4 %scatter_custom_fusion = f32[6,1024]{0,1:T(8,128)S(1)} fusion(s32[3072]{0:T(1024)S(1)} %bitcast.549, f32[3072,6]{1,0:T(8,128)} %copy.972, f32[]{:T(128)} %constant.32.clone.1), kind=kCustom, calls=%fused_computation.42 | custom fusion | flops 18432 | bytes 25088 | tf_op jit(solution)/shard_map/scatter-add | solution.py:149
  134.8 18.9 %scatter_fusion = f32[6,1024]{0,1:T(8,128)S(1)} fusion(f32[6,1024]{0,1:T(8,128)S(1)} %scatter_custom_fusion, s32[3072]{0:T(1024)S(1)} %bitcast.494, f32[3072,6]{1,0:T(8,128)S(1)} %copy.973), kind=kCustom, calls=%fused_computation.23 | custom fusion | flops 18432 | bytes 233472 | tf_op jit(solution)/shard_map/scatter-add | solution.py:150
  184.6 12.6 %all-reduce.15 = (f32[]{:T(128)}, f32[]{:T(128)}) all-reduce(f32[]{:T(128)} %get-tuple-element.40, f32[]{:T(128)} %get-tuple-element.39), channel_id=1, replica_groups=mesh['gx'=4,'gy_0'=4,'gy_1'=2,'gz_0'=4,'gz_1'=4] {'gx'}, use_global_device_ids=true, to_apply=%region_1.2 | all-reduce | flops 2 | bytes 16 | tf_op jit(solution)/shard_map/psum | solution.py:16
  197.1 9.2 %all-reduce.11 = (f32[]{:T(128)}, f32[]{:T(128)}) all-reduce(f32[]{:T(128)} %get-tuple-element.85, f32[]{:T(128)} %get-tuple-element.86), channel_id=1, replica_groups=mesh['gx'=4,'gy_0'=4,'gy_1'=2,'gz_0'=4,'gz_1'=4] {'gy_0'}, use_global_device_ids=true, to_apply=%region_2.3 | all-reduce | flops 2 | bytes 16 | tf_op jit(solution)/shard_map/psum | solution.py:16
  220.2 13.1 %all-reduce.3 = (f32[]{:T(128)}, f32[]{:T(128)}) all-reduce(f32[]{:T(128)} %get-tuple-element.69, f32[]{:T(128)} %get-tuple-element.70), channel_id=1, replica_groups=mesh['gx'=4,'gy_0'=4,'gy_1'=2,'gz_0'=4,'gz_1'=4] {'gz_1'}, use_global_device_ids=true, to_apply=%region_5.6 | all-reduce | flops 2 | bytes 16 | tf_op jit(solution)/shard_map/psum | solution.py:16
  253.0 8.1 %gather_fusion.9 = f32[3072,6]{1,0:T(8,128)S(1)} fusion(f32[6,1024]{0,1:T(8,128)S(1)} %copy.993, s32[3072]{0:T(1024)S(1)} %get-tuple-element.239), kind=kCustom, calls=%fused_computation.9 | custom fusion | bytes 159744 | tf_op jit(solution)/shard_map/gather | solution.py:146
  269.1 8.1 %gather_fusion.8 = f32[3072,6]{1,0:T(8,128)S(1)} fusion(f32[6,1024]{0,1:T(8,128)S(1)} %copy.993, s32[3072]{0:T(1024)S(1)} %get-tuple-element.240), kind=kCustom, calls=%fused_computation.8 | custom fusion | bytes 159744 | tf_op jit(solution)/shard_map/gather | solution.py:147
  284.3 10.1 %gather_fusion.7 = f32[3072,6]{1,0:T(8,128)S(1)} fusion(f32[6,6912]{0,1:T(8,128)} %bitcast.458, s32[3072]{0:T(1024)S(1)} %broadcast_clamp_fusion.2), kind=kCustom, calls=%fused_computation.7 | custom fusion | bytes 159744 | tf_op jit(solution)/shard_map/gather | solution.py:147
  296.6 17.0 %scatter_custom_fusion.3 = f32[6,1024]{0,1:T(8,128)S(1)} fusion(s32[3072]{0:T(1024)S(1)} %bitcast.550, f32[3072,6]{1,0:T(8,128)S(1)} %copy.998, f32[]{:T(128)} %constant.32.clone.1), kind=kCustom, calls=%fused_computation.40 | custom fusion | flops 18432 | bytes 24580 | tf_op jit(solution)/shard_map/scatter-add | solution.py:149
  314.2 18.4 %scatter_fusion.2 = f32[6,1024]{0,1:T(8,128)S(1)} fusion(f32[6,1024]{0,1:T(8,128)S(1)} %scatter_custom_fusion.3, s32[3072]{0:T(1024)S(1)} %bitcast.495, f32[3072,6]{1,0:T(8,128)S(1)} %copy.999), kind=kCustom, calls=%fused_computation.26 | custom fusion | flops 18432 | bytes 233472 | tf_op jit(solution)/shard_map/scatter-add | solution.py:150
  339.8 12.7 %all-reduce.14 = (f32[]{:T(128)}, f32[]{:T(128)}) all-reduce(f32[]{:T(128)} %get-tuple-element.36, f32[]{:T(128)} %get-tuple-element.35), channel_id=1, replica_groups=mesh['gx'=4,'gy_0'=4,'gy_1'=2,'gz_0'=4,'gz_1'=4] {'gx'}, use_global_device_ids=true, to_apply=%region_20.21 | all-reduce | flops 2 | bytes 16 | tf_op jit(solution)/shard_map/psum | solution.py:16
  352.4 9.5 %all-reduce.10 = (f32[]{:T(128)}, f32[]{:T(128)}) all-reduce(f32[]{:T(128)} %get-tuple-element.83, f32[]{:T(128)} %get-tuple-element.84), channel_id=1, replica_groups=mesh['gx'=4,'gy_0'=4,'gy_1'=2,'gz_0'=4,'gz_1'=4] {'gy_0'}, use_global_device_ids=true, to_apply=%region_21.22 | all-reduce | flops 2 | bytes 16 | tf_op jit(solution)/shard_map/psum | solution.py:16
  373.8 11.1 %all-reduce.2 = (f32[]{:T(128)}, f32[]{:T(128)}) all-reduce(f32[]{:T(128)} %get-tuple-element.67, f32[]{:T(128)} %get-tuple-element.68), channel_id=1, replica_groups=mesh['gx'=4,'gy_0'=4,'gy_1'=2,'gz_0'=4,'gz_1'=4] {'gz_1'}, use_global_device_ids=true, to_apply=%region_24.25 | all-reduce | flops 2 | bytes 16 | tf_op jit(solution)/shard_map/psum | solution.py:16
  409.1 8.1 %gather_fusion.14 = f32[3072,6]{1,0:T(8,128)S(1)} fusion(f32[6,1024]{0,1:T(8,128)S(1)} %copy.1012, s32[3072]{0:T(1024)S(1)} %get-tuple-element.239), kind=kCustom, calls=%fused_computation.14 | custom fusion | bytes 159744 | tf_op jit(solution)/shard_map/gather | solution.py:146
  425.2 8.1 %gather_fusion.13 = f32[3072,6]{1,0:T(8,128)S(1)} fusion(f32[6,1024]{0,1:T(8,128)S(1)} %copy.1012, s32[3072]{0:T(1024)S(1)} %get-tuple-element.240), kind=kCustom, calls=%fused_computation.13 | custom fusion | bytes 159744 | tf_op jit(solution)/shard_map/gather | solution.py:147
  440.5 10.1 %gather_fusion.12 = f32[3072,6]{1,0:T(8,128)S(1)} fusion(f32[6,6912]{0,1:T(8,128)} %bitcast.460, s32[3072]{0:T(1024)S(1)} %broadcast_clamp_fusion.2), kind=kCustom, calls=%fused_computation.12 | custom fusion | bytes 159744 | tf_op jit(solution)/shard_map/gather | solution.py:147
  452.8 17.0 %scatter_custom_fusion.6 = f32[6,1024]{0,1:T(8,128)S(1)} fusion(s32[3072]{0:T(1024)S(1)} %bitcast.551, f32[3072,6]{1,0:T(8,128)S(1)} %copy.1017, f32[]{:T(128)} %constant.32.clone.1), kind=kCustom, calls=%fused_computation.38 | custom fusion | flops 18432 | bytes 24580 | tf_op jit(solution)/shard_map/scatter-add | solution.py:149
  470.4 18.4 %scatter_fusion.4 = f32[6,1024]{0,1:T(8,128)S(1)} fusion(f32[6,1024]{0,1:T(8,128)S(1)} %scatter_custom_fusion.6, s32[3072]{0:T(1024)S(1)} %bitcast.496, f32[3072,6]{1,0:T(8,128)S(1)} %copy.1018), kind=kCustom, calls=%fused_computation.29 | custom fusion | flops 18432 | bytes 233472 | tf_op jit(solution)/shard_map/scatter-add | solution.py:150
  495.9 12.6 %all-reduce.13 = (f32[]{:T(128)}, f32[]{:T(128)}) all-reduce(f32[]{:T(128)} %get-tuple-element.34, f32[]{:T(128)} %get-tuple-element.33), channel_id=1, replica_groups=mesh['gx'=4,'gy_0'=4,'gy_1'=2,'gz_0'=4,'gz_1'=4] {'gx'}, use_global_device_ids=true, to_apply=%region_39.40 | all-reduce | flops 2 | bytes 16 | tf_op jit(solution)/shard_map/psum | solution.py:16
  529.7 11.1 %all-reduce.1 = (f32[]{:T(128)}, f32[]{:T(128)}) all-reduce(f32[]{:T(128)} %get-tuple-element.65, f32[]{:T(128)} %get-tuple-element.66), channel_id=1, replica_groups=mesh['gx'=4,'gy_0'=4,'gy_1'=2,'gz_0'=4,'gz_1'=4] {'gz_1'}, use_global_device_ids=true, to_apply=%region_43.44 | all-reduce | flops 2 | bytes 16 | tf_op jit(solution)/shard_map/psum | solution.py:16
  563.0 8.1 %gather_fusion.19 = f32[3072,6]{1,0:T(8,128)S(1)} fusion(f32[6,1024]{0,1:T(8,128)S(1)} %copy.1031, s32[3072]{0:T(1024)S(1)} %get-tuple-element.239), kind=kCustom, calls=%fused_computation.19 | custom fusion | bytes 159744 | tf_op jit(solution)/shard_map/gather | solution.py:146
  579.2 8.1 %gather_fusion.18 = f32[3072,6]{1,0:T(8,128)S(1)} fusion(f32[6,1024]{0,1:T(8,128)S(1)} %copy.1031, s32[3072]{0:T(1024)S(1)} %get-tuple-element.240), kind=kCustom, calls=%fused_computation.18 | custom fusion | bytes 159744 | tf_op jit(solution)/shard_map/gather | solution.py:147
  594.4 10.1 %gather_fusion.17 = f32[3072,6]{1,0:T(8,128)S(1)} fusion(f32[6,6912]{0,1:T(8,128)} %bitcast.456, s32[3072]{0:T(1024)S(1)} %broadcast_clamp_fusion.2), kind=kCustom, calls=%fused_computation.17 | custom fusion | bytes 159744 | tf_op jit(solution)/shard_map/gather | solution.py:147
  606.7 17.0 %scatter_custom_fusion.9 = f32[6,1024]{0,1:T(8,128)S(1)} fusion(s32[3072]{0:T(1024)S(1)} %bitcast.552, f32[3072,6]{1,0:T(8,128)S(1)} %copy.1036, f32[]{:T(128)} %constant.32.clone.1), kind=kCustom, calls=%fused_computation.36 | custom fusion | flops 18432 | bytes 24580 | tf_op jit(solution)/shard_map/scatter-add | solution.py:149
  624.3 18.4 %scatter_fusion.6 = f32[6,1024]{0,1:T(8,128)S(1)} fusion(f32[6,1024]{0,1:T(8,128)S(1)} %scatter_custom_fusion.9, s32[3072]{0:T(1024)S(1)} %bitcast.497, f32[3072,6]{1,0:T(8,128)S(1)} %copy.1037), kind=kCustom, calls=%fused_computation.32 | custom fusion | flops 18432 | bytes 233472 | tf_op jit(solution)/shard_map/scatter-add | solution.py:150
  649.8 12.7 %all-reduce.12 = (f32[]{:T(128)}, f32[]{:T(128)}) all-reduce(f32[]{:T(128)} %get-tuple-element.32, f32[]{:T(128)} %get-tuple-element.31), channel_id=1, replica_groups=mesh['gx'=4,'gy_0'=4,'gy_1'=2,'gz_0'=4,'gz_1'=4] {'gx'}, use_global_device_ids=true, to_apply=%region_58.59 | all-reduce | flops 2 | bytes 16 | tf_op jit(solution)/shard_map/psum | solution.py:16
  662.5 9.4 %all-reduce.8 = (f32[]{:T(128)}, f32[]{:T(128)}) all-reduce(f32[]{:T(128)} %get-tuple-element.79, f32[]{:T(128)} %get-tuple-element.80), channel_id=1, replica_groups=mesh['gx'=4,'gy_0'=4,'gy_1'=2,'gz_0'=4,'gz_1'=4] {'gy_0'}, use_global_device_ids=true, to_apply=%region_59.60 | all-reduce | flops 2 | bytes 16 | tf_op jit(solution)/shard_map/psum | solution.py:16
  683.7 11.1 %all-reduce = (f32[]{:T(128)}, f32[]{:T(128)}) all-reduce(f32[]{:T(128)} %get-tuple-element.63, f32[]{:T(128)} %get-tuple-element.64), channel_id=1, replica_groups=mesh['gx'=4,'gy_0'=4,'gy_1'=2,'gz_0'=4,'gz_1'=4] {'gz_1'}, use_global_device_ids=true, to_apply=%region_62.63 | all-reduce | flops 2 | bytes 16 | tf_op jit(solution)/shard_map/psum | solution.py:16
  (328 shorter events, 297.8 us)
Async XLA Ops:
  2.9 61.3 %collective-permute-start.7 = (s32[1,1,1,3,832]{4,3,2,1,0:T(4,128)S(1)}, s32[1,1,1,3,832]{4,3,2,1,0:T(4,128)S(1)}, u32[]{:S(2)}, u32[]{:S(2)}) collective-permute-start(s32[1,1,1,3,832]{4,3,2,1,0:T(4,128)S(1)} %add_bitcast_fusion.1), channel_id=1, source_target_pairs={{128,0},{256,128},{384,256},{0,384},{129,1},{257,129},{385,257},{1... | collective-permute-start | bytes 29960 | tf_op jit(solution)/shard_map/ppermute | solution.py:29
  16.2 48.8 %collective-permute-start.6 = (s32[1,1,1,3,832]{4,3,2,1,0:T(4,128)S(1)}, s32[1,1,1,3,832]{4,3,2,1,0:T(4,128)S(1)}, u32[]{:S(2)}, u32[]{:S(2)}) collective-permute-start(s32[1,1,1,3,832]{4,3,2,1,0:T(4,128)S(1)} %add_bitcast_fusion.1), channel_id=1, source_target_pairs={{0,128},{128,256},{256,384},{384,0},{1,129},{129,257},{257,385},{3... | collective-permute-start | bytes 29960 | tf_op jit(solution)/shard_map/ppermute | solution.py:26
  18.9 42.8 %collective-permute-start.1 = (f32[1,1,1,6,256]{4,3,2,1,0:T(8,128)S(1)}, f32[1,1,1,6,256]{4,3,2,1,0:T(8,128)S(1)}, u32[]{:S(2)}, u32[]{:S(2)}) collective-permute-start(f32[1,1,1,6,256]{4,3,2,1,0:T(8,128)S(1)} %slice_bitcast_fusion.5), channel_id=1, source_target_pairs={{128,0},{256,128},{384,256},{0,384},{129,1},{257,129},{385,257},{1... | collective-permute-start | bytes 18440 | tf_op jit(solution)/shard_map/ppermute | solution.py:29
  26.2 33.5 %collective-permute-start = (f32[1,1,1,6,256]{4,3,2,1,0:T(8,128)S(1)}, f32[1,1,1,6,256]{4,3,2,1,0:T(8,128)S(1)}, u32[]{:S(2)}, u32[]{:S(2)}) collective-permute-start(f32[1,1,1,6,256]{4,3,2,1,0:T(8,128)S(1)} %slice_bitcast_fusion.5), channel_id=1, source_target_pairs={{0,128},{128,256},{256,384},{384,0},{1,129},{129,257},{257,385},{3... | collective-permute-start | bytes 18440 | tf_op jit(solution)/shard_map/ppermute | solution.py:26
  29.8 43.2 %collective-permute-start.13 = (f32[1,1,1,5,832]{4,3,2,1,0:T(8,128)S(1)}, f32[1,1,1,5,832]{4,3,2,1,0:T(8,128)S(1)}, u32[]{:S(2)}, u32[]{:S(2)}) collective-permute-start(f32[1,1,1,5,832]{4,3,2,1,0:T(8,128)S(1)} %maximum_bitcast_fusion.4), channel_id=1, source_target_pairs={{128,0},{256,128},{384,256},{0,384},{129,1},{257,129},{385,257},{1... | collective-permute-start | bytes 49928 | tf_op jit(solution)/shard_map/ppermute | solution.py:29
  61.7 11.4 %collective-permute-start.3 = (f32[3,1,1,6,256]{4,2,3,1,0:T(1,128)S(1)}, f32[3,1,1,6,256]{4,2,3,1,0:T(1,128)S(1)}, u32[]{:S(2)}, u32[]{:S(2)}) collective-permute-start(f32[3,1,1,6,256]{4,2,3,1,0:T(1,128)S(1)} %constant_dynamic-update-slice_fusion), channel_id=1, source_target_pairs={{16,0},{32,16},{48,32},{64,48},{80,64},{96,80},{112,96},{0,112},{1... | collective-permute-start | bytes 55304 | tf_op jit(solution)/shard_map/ppermute | solution.py:29
  64.2 10.6 %collective-permute-start.2 = (f32[3,1,1,6,256]{4,2,3,1,0:T(1,128)S(1)}, f32[3,1,1,6,256]{4,2,3,1,0:T(1,128)S(1)}, u32[]{:S(2)}, u32[]{:S(2)}) collective-permute-start(f32[3,1,1,6,256]{4,2,3,1,0:T(1,128)S(1)} %constant_dynamic-update-slice_fusion), channel_id=1, source_target_pairs={{0,16},{16,32},{32,48},{48,64},{64,80},{80,96},{96,112},{112,0},{1... | collective-permute-start | bytes 55304 | tf_op jit(solution)/shard_map/ppermute | solution.py:26
  65.0 15.3 %collective-permute-start.9 = (s32[3,1,1,3,832]{4,3,2,1,0:T(4,128)S(1)}, s32[3,1,1,3,832]{4,3,2,1,0:T(4,128)S(1)}, u32[]{:S(2)}, u32[]{:S(2)}) collective-permute-start(s32[3,1,1,3,832]{4,3,2,1,0:T(4,128)S(1)} %pad_add_fusion.2), channel_id=1, source_target_pairs={{16,0},{32,16},{48,32},{64,48},{80,64},{96,80},{112,96},{0,112},{1... | collective-permute-start | bytes 89864 | tf_op jit(solution)/shard_map/ppermute | solution.py:29
  68.2 14.0 %collective-permute-start.8 = (s32[3,1,1,3,832]{4,3,2,1,0:T(4,128)S(1)}, s32[3,1,1,3,832]{4,3,2,1,0:T(4,128)S(1)}, u32[]{:S(2)}, u32[]{:S(2)}) collective-permute-start(s32[3,1,1,3,832]{4,3,2,1,0:T(4,128)S(1)} %pad_add_fusion.2), channel_id=1, source_target_pairs={{0,16},{16,32},{32,48},{48,64},{64,80},{80,96},{96,112},{112,0},{1... | collective-permute-start | bytes 89864 | tf_op jit(solution)/shard_map/ppermute | solution.py:26
  73.0 16.6 %collective-permute-start.15 = (f32[3,1,1,5,832]{4,2,3,1,0:T(1,128)S(1)}, f32[3,1,1,5,832]{4,2,3,1,0:T(1,128)S(1)}, u32[]{:S(2)}, u32[]{:S(2)}) collective-permute-start(f32[3,1,1,5,832]{4,2,3,1,0:T(1,128)S(1)} %constant_dynamic-update-slice_fusion.3), channel_id=1, source_target_pairs={{16,0},{32,16},{48,32},{64,48},{80,64},{96,80},{112,96},{0,112},{1... | collective-permute-start | bytes 149768 | tf_op jit(solution)/shard_map/ppermute | solution.py:29
  73.1 18.5 %collective-permute-start.14 = (f32[3,1,1,5,832]{4,2,3,1,0:T(1,128)S(1)}, f32[3,1,1,5,832]{4,2,3,1,0:T(1,128)S(1)}, u32[]{:S(2)}, u32[]{:S(2)}) collective-permute-start(f32[3,1,1,5,832]{4,2,3,1,0:T(1,128)S(1)} %constant_dynamic-update-slice_fusion.3), channel_id=1, source_target_pairs={{0,16},{16,32},{32,48},{48,64},{64,80},{80,96},{96,112},{112,0},{1... | collective-permute-start | bytes 149768 | tf_op jit(solution)/shard_map/ppermute | solution.py:26
  74.8 24.8 %collective-permute-start.5 = (f32[3,3,1,6,256]{4,2,3,1,0:T(1,128)S(1)}, f32[3,3,1,6,256]{4,2,3,1,0:T(1,128)S(1)}, u32[]{:S(2)}, u32[]{:S(2)}) collective-permute-start(f32[3,3,1,6,256]{4,2,3,1,0:T(1,128)S(1)} %pad_maximum_fusion.6), channel_id=1, source_target_pairs={{1,0},{2,1},{3,2},{4,3},{5,4},{6,5},{7,6},{8,7},{9,8},{10,9},{11,1... | collective-permute-start | bytes 165896 | tf_op jit(solution)/shard_map/ppermute | solution.py:29
  80.3 21.2 %collective-permute-start.4 = (f32[3,3,1,6,256]{4,2,3,1,0:T(1,128)S(1)}, f32[3,3,1,6,256]{4,2,3,1,0:T(1,128)S(1)}, u32[]{:S(2)}, u32[]{:S(2)}) collective-permute-start(f32[3,3,1,6,256]{4,2,3,1,0:T(1,128)S(1)} %pad_maximum_fusion.6), channel_id=1, source_target_pairs={{0,1},{1,2},{2,3},{3,4},{4,5},{5,6},{6,7},{7,8},{8,9},{9,10},{10,1... | collective-permute-start | bytes 165896 | tf_op jit(solution)/shard_map/ppermute | solution.py:26
  82.3 71.4 %collective-permute-start.11 = (s32[3,3,1,3,832]{4,3,2,1,0:T(4,128)S(1)}, s32[3,3,1,3,832]{4,3,2,1,0:T(4,128)}, u32[]{:S(2)}, u32[]{:S(2)}) collective-permute-start(s32[3,3,1,3,832]{4,3,2,1,0:T(4,128)S(1)} %pad_add_fusion.1), channel_id=1, source_target_pairs={{1,0},{2,1},{3,2},{4,3},{5,4},{6,5},{7,6},{8,7},{9,8},{10,9},{11,1... | collective-permute-start | bytes 269576 | tf_op jit(solution)/shard_map/ppermute | solution.py:29
  89.6 64.2 %collective-permute-start.10 = (s32[3,3,1,3,832]{4,3,2,1,0:T(4,128)S(1)}, s32[3,3,1,3,832]{4,3,2,1,0:T(4,128)}, u32[]{:S(2)}, u32[]{:S(2)}) collective-permute-start(s32[3,3,1,3,832]{4,3,2,1,0:T(4,128)S(1)} %pad_add_fusion.1), channel_id=1, source_target_pairs={{0,1},{1,2},{2,3},{3,4},{4,5},{5,6},{6,7},{7,8},{8,9},{9,10},{10,1... | collective-permute-start | bytes 269576 | tf_op jit(solution)/shard_map/ppermute | solution.py:26
  92.3 74.1 %collective-permute-start.17 = (f32[3,3,1,5,832]{4,2,3,1,0:T(1,128)}, f32[3,3,1,5,832]{4,2,3,1,0:T(1,128)}, u32[]{:S(2)}, u32[]{:S(2)}) collective-permute-start(f32[3,3,1,5,832]{4,2,3,1,0:T(1,128)} %pad_maximum_fusion.5), channel_id=1, source_target_pairs={{1,0},{2,1},{3,2},{4,3},{5,4},{6,5},{7,6},{8,7},{9,8},{10,9},{11,1... | collective-permute-start | bytes 449288 | tf_op jit(solution)/shard_map/ppermute | solution.py:29
  99.6 66.8 %collective-permute-start.16 = (f32[3,3,1,5,832]{4,2,3,1,0:T(1,128)}, f32[3,3,1,5,832]{4,2,3,1,0:T(1,128)}, u32[]{:S(2)}, u32[]{:S(2)}) collective-permute-start(f32[3,3,1,5,832]{4,2,3,1,0:T(1,128)} %pad_maximum_fusion.5), channel_id=1, source_target_pairs={{0,1},{1,2},{2,3},{3,4},{4,5},{5,6},{6,7},{7,8},{8,9},{9,10},{10,1... | collective-permute-start | bytes 449288 | tf_op jit(solution)/shard_map/ppermute | solution.py:26
  234.6 9.2 %collective-permute-start.18 = (f32[1,1,1,6,256]{4,3,2,1,0:T(8,128)S(1)}, f32[1,1,1,6,256]{4,3,2,1,0:T(8,128)S(1)}, u32[]{:S(2)}, u32[]{:S(2)}) collective-permute-start(f32[1,1,1,6,256]{4,3,2,1,0:T(8,128)S(1)} %slice_bitcast_fusion.4), channel_id=1, source_target_pairs={{0,128},{128,256},{256,384},{384,0},{1,129},{129,257},{257,385},{3... | collective-permute-start | bytes 18440 | tf_op jit(solution)/shard_map/ppermute | solution.py:26
  246.9 14.7 %collective-permute-start.21 = (f32[3,1,1,6,256]{4,2,3,1,0:T(1,128)S(1)}, f32[3,1,1,6,256]{4,2,3,1,0:T(1,128)S(1)}, u32[]{:S(2)}, u32[]{:S(2)}) collective-permute-start(f32[3,1,1,6,256]{4,2,3,1,0:T(1,128)S(1)} %constant_dynamic-update-slice_fusion.6), channel_id=1, source_target_pairs={{16,0},{32,16},{48,32},{64,48},{80,64},{96,80},{112,96},{0,112},{1... | collective-permute-start | bytes 55304 | tf_op jit(solution)/shard_map/ppermute | solution.py:29
  252.7 8.8 %collective-permute-start.20 = (f32[3,1,1,6,256]{4,2,3,1,0:T(1,128)S(1)}, f32[3,1,1,6,256]{4,2,3,1,0:T(1,128)S(1)}, u32[]{:S(2)}, u32[]{:S(2)}) collective-permute-start(f32[3,1,1,6,256]{4,2,3,1,0:T(1,128)S(1)} %constant_dynamic-update-slice_fusion.6), channel_id=1, source_target_pairs={{0,16},{16,32},{32,48},{48,64},{64,80},{80,96},{96,112},{112,0},{1... | collective-permute-start | bytes 55304 | tf_op jit(solution)/shard_map/ppermute | solution.py:26
  261.7 16.2 %collective-permute-start.23 = (f32[3,3,1,6,256]{4,2,3,1,0:T(1,128)S(1)}, f32[3,3,1,6,256]{4,2,3,1,0:T(1,128)S(1)}, u32[]{:S(2)}, u32[]{:S(2)}) collective-permute-start(f32[3,3,1,6,256]{4,2,3,1,0:T(1,128)S(1)} %pad_maximum_fusion.7), channel_id=1, source_target_pairs={{1,0},{2,1},{3,2},{4,3},{5,4},{6,5},{7,6},{8,7},{9,8},{10,9},{11,1... | collective-permute-start | bytes 165896 | tf_op jit(solution)/shard_map/ppermute | solution.py:29
  263.6 14.3 %collective-permute-start.22 = (f32[3,3,1,6,256]{4,2,3,1,0:T(1,128)S(1)}, f32[3,3,1,6,256]{4,2,3,1,0:T(1,128)S(1)}, u32[]{:S(2)}, u32[]{:S(2)}) collective-permute-start(f32[3,3,1,6,256]{4,2,3,1,0:T(1,128)S(1)} %pad_maximum_fusion.7), channel_id=1, source_target_pairs={{0,1},{1,2},{2,3},{3,4},{4,5},{5,6},{6,7},{7,8},{8,9},{9,10},{10,1... | collective-permute-start | bytes 165896 | tf_op jit(solution)/shard_map/ppermute | solution.py:26
  389.3 9.2 %collective-permute-start.24 = (f32[1,1,1,6,256]{4,3,2,1,0:T(8,128)S(1)}, f32[1,1,1,6,256]{4,3,2,1,0:T(8,128)S(1)}, u32[]{:S(2)}, u32[]{:S(2)}) collective-permute-start(f32[1,1,1,6,256]{4,3,2,1,0:T(8,128)S(1)} %slice_bitcast_fusion.3), channel_id=1, source_target_pairs={{0,128},{128,256},{256,384},{384,0},{1,129},{129,257},{257,385},{3... | collective-permute-start | bytes 18440 | tf_op jit(solution)/shard_map/ppermute | solution.py:26
  401.6 16.1 %collective-permute-start.27 = (f32[3,1,1,6,256]{4,2,3,1,0:T(1,128)S(1)}, f32[3,1,1,6,256]{4,2,3,1,0:T(1,128)S(1)}, u32[]{:S(2)}, u32[]{:S(2)}) collective-permute-start(f32[3,1,1,6,256]{4,2,3,1,0:T(1,128)S(1)} %constant_dynamic-update-slice_fusion.9), channel_id=1, source_target_pairs={{16,0},{32,16},{48,32},{64,48},{80,64},{96,80},{112,96},{0,112},{1... | collective-permute-start | bytes 55304 | tf_op jit(solution)/shard_map/ppermute | solution.py:29
  407.5 10.3 %collective-permute-start.26 = (f32[3,1,1,6,256]{4,2,3,1,0:T(1,128)S(1)}, f32[3,1,1,6,256]{4,2,3,1,0:T(1,128)S(1)}, u32[]{:S(2)}, u32[]{:S(2)}) collective-permute-start(f32[3,1,1,6,256]{4,2,3,1,0:T(1,128)S(1)} %constant_dynamic-update-slice_fusion.9), channel_id=1, source_target_pairs={{0,16},{16,32},{32,48},{48,64},{64,80},{80,96},{96,112},{112,0},{1... | collective-permute-start | bytes 55304 | tf_op jit(solution)/shard_map/ppermute | solution.py:26
  417.8 16.3 %collective-permute-start.29 = (f32[3,3,1,6,256]{4,2,3,1,0:T(1,128)S(1)}, f32[3,3,1,6,256]{4,2,3,1,0:T(1,128)S(1)}, u32[]{:S(2)}, u32[]{:S(2)}) collective-permute-start(f32[3,3,1,6,256]{4,2,3,1,0:T(1,128)S(1)} %pad_maximum_fusion.8), channel_id=1, source_target_pairs={{1,0},{2,1},{3,2},{4,3},{5,4},{6,5},{7,6},{8,7},{9,8},{10,9},{11,1... | collective-permute-start | bytes 165896 | tf_op jit(solution)/shard_map/ppermute | solution.py:29
  419.7 14.4 %collective-permute-start.28 = (f32[3,3,1,6,256]{4,2,3,1,0:T(1,128)S(1)}, f32[3,3,1,6,256]{4,2,3,1,0:T(1,128)S(1)}, u32[]{:S(2)}, u32[]{:S(2)}) collective-permute-start(f32[3,3,1,6,256]{4,2,3,1,0:T(1,128)S(1)} %pad_maximum_fusion.8), channel_id=1, source_target_pairs={{0,1},{1,2},{2,3},{3,4},{4,5},{5,6},{6,7},{7,8},{8,9},{9,10},{10,1... | collective-permute-start | bytes 165896 | tf_op jit(solution)/shard_map/ppermute | solution.py:26
  544.6 9.2 %collective-permute-start.30 = (f32[1,1,1,6,256]{4,3,2,1,0:T(8,128)S(1)}, f32[1,1,1,6,256]{4,3,2,1,0:T(8,128)S(1)}, u32[]{:S(2)}, u32[]{:S(2)}) collective-permute-start(f32[1,1,1,6,256]{4,3,2,1,0:T(8,128)S(1)} %slice_bitcast_fusion.2), channel_id=1, source_target_pairs={{0,128},{128,256},{256,384},{384,0},{1,129},{129,257},{257,385},{3... | collective-permute-start | bytes 18440 | tf_op jit(solution)/shard_map/ppermute | solution.py:26
  556.9 14.7 %collective-permute-start.33 = (f32[3,1,1,6,256]{4,2,3,1,0:T(1,128)S(1)}, f32[3,1,1,6,256]{4,2,3,1,0:T(1,128)S(1)}, u32[]{:S(2)}, u32[]{:S(2)}) collective-permute-start(f32[3,1,1,6,256]{4,2,3,1,0:T(1,128)S(1)} %constant_dynamic-update-slice_fusion.12), channel_id=1, source_target_pairs={{16,0},{32,16},{48,32},{64,48},{80,64},{96,80},{112,96},{0,112},{1... | collective-permute-start | bytes 55304 | tf_op jit(solution)/shard_map/ppermute | solution.py:29
  562.8 8.8 %collective-permute-start.32 = (f32[3,1,1,6,256]{4,2,3,1,0:T(1,128)S(1)}, f32[3,1,1,6,256]{4,2,3,1,0:T(1,128)S(1)}, u32[]{:S(2)}, u32[]{:S(2)}) collective-permute-start(f32[3,1,1,6,256]{4,2,3,1,0:T(1,128)S(1)} %constant_dynamic-update-slice_fusion.12), channel_id=1, source_target_pairs={{0,16},{16,32},{32,48},{48,64},{64,80},{80,96},{96,112},{112,0},{1... | collective-permute-start | bytes 55304 | tf_op jit(solution)/shard_map/ppermute | solution.py:26
  571.7 16.3 %collective-permute-start.35 = (f32[3,3,1,6,256]{4,2,3,1,0:T(1,128)S(1)}, f32[3,3,1,6,256]{4,2,3,1,0:T(1,128)S(1)}, u32[]{:S(2)}, u32[]{:S(2)}) collective-permute-start(f32[3,3,1,6,256]{4,2,3,1,0:T(1,128)S(1)} %pad_maximum_fusion.9), channel_id=1, source_target_pairs={{1,0},{2,1},{3,2},{4,3},{5,4},{6,5},{7,6},{8,7},{9,8},{10,9},{11,1... | collective-permute-start | bytes 165896 | tf_op jit(solution)/shard_map/ppermute | solution.py:29
  573.6 14.4 %collective-permute-start.34 = (f32[3,3,1,6,256]{4,2,3,1,0:T(1,128)S(1)}, f32[3,3,1,6,256]{4,2,3,1,0:T(1,128)S(1)}, u32[]{:S(2)}, u32[]{:S(2)}) collective-permute-start(f32[3,3,1,6,256]{4,2,3,1,0:T(1,128)S(1)} %pad_maximum_fusion.9), channel_id=1, source_target_pairs={{0,1},{1,2},{2,3},{3,4},{4,5},{5,6},{6,7},{7,8},{8,9},{9,10},{10,1... | collective-permute-start | bytes 165896 | tf_op jit(solution)/shard_map/ppermute | solution.py:26
  (10 other events, 80.4 us)
where the time goes:
time: 712 us; the launch traced here: 701 us
  blocking collectives  184 us (26%)
  other arithmetic  180 us (25%)
  local copies, waits for them, and re-layouts  176 us (25%)
  starting transfers between devices  132 us (19%)
  between operations  16.5 us (2%)
  waiting for transfers between devices  12.4 us (2%)
    psum x20, blocking collectives, one_axis_at_a_time(): value = lax.psum(value, axis)  184 us
    ppermute x18, starting transfers between devices, with_halo(): lax.ppermute(lax.slice_in_dim(block, 0, width, axis=dim), axis, backward)  89.2 us
    scatter-add x4, other arithmetic, operate(): forces.at[:, near_grain].add(jnp.where(far_slot[None], 0.0, on_second))  74.2 us
    scatter-add x4, other arithmetic, operate(): forces = jnp.zeros_like(field).at[:, owners].add(on_first)  68.5 us
    ppermute x18, starting transfers between devices, with_halo(): lax.ppermute(lax.slice_in_dim(block, block.shape[dim] - width, None, axis...  42.9 us
    gather x8, local copies, waits for them, and re-layouts, operate(): rim_flat[:, ghost_column]  42.3 us
    gather x8, local copies, waits for them, and re-layouts, operate(): field[:, near_grain]  34.5 us
    gather x8, local copies, waits for them, and re-layouts, operate(): first_u = field[:, owners]  34.4 us
  transfers between devices with their start and end apart: 36, of which 4 were waited for; matrix products, arithmetic and copies ran while one was open for 21% of the time, Pallas kernels for 0%

commit v1 on v0

v1 whole, which is shorter than its diff:
```python
import functools

import jax
import jax.numpy as jnp
from jax import lax
from jax.experimental import pallas as pl
from jax.experimental.pallas import tpu as pltpu
from jax.sharding import PartitionSpec as P

F32 = jnp.float32
BF16 = jnp.bfloat16
MESH = pl.DeviceIdType.MESH
GRAINS = 1024
RIM = 256
NEAR = 2240
TYPES = 4
SIDES = 26
LOCAL_ROWS = 18
NX, NY, NZ = 4, 8, 16
ZLO = 4
PLANE = 32
LINE = 16


def offset_of(side):
    whole = side + (1 if side >= 13 else 0)
    return (whole // 9 - 1, whole // 3 % 3 - 1, whole % 3 - 1)


def cross(w, n):
    return [
        w[1] * n[2] - w[2] * n[1],
        w[2] * n[0] - w[0] * n[2],
        w[0] * n[1] - w[1] * n[0],
    ]


def response(a, b, n, ra, rb, coeff, both):
    shear, normal_less, roll, twist_less = coeff
    arm = [rb * b[3 + c] + ra * a[3 + c] for c in range(3)]
    turn = cross(arm, n)
    delta = [b[c] - a[c] - turn[c] for c in range(3)]
    along = normal_less * (n[0] * delta[0] + n[1] * delta[1] + n[2] * delta[2])
    force = [shear * delta[c] + along * n[c] for c in range(3)]
    theta = [b[3 + c] - a[3 + c] for c in range(3)]
    twist = twist_less * (n[0] * theta[0] + n[1] * theta[1] + n[2] * theta[2])
    moment = [roll * theta[c] + twist * n[c] for c in range(3)]
    lever = cross(n, force)
    first = force + [ra * lever[c] + moment[c] for c in range(3)]
    if not both:
        return first, None
    second = [-f for f in force] + [rb * lever[c] - moment[c] for c in range(3)]
    return first, second


def lanes(x, index):
    return jnp.take_along_axis(x, index, axis=1, mode="promise_in_bounds")


def splat(row):
    return jnp.broadcast_to(row, (8, 128))


def kernel(
    rhs_ref, diag_ref, stiff_ref, own_ref, slot_ref, type_ref, normal_ref, radii_ref,
    x_ref, r_ref,
    dense, idx_a, idx_b, geo, one_hot, t_local, lhs_local,
    rim_idx, rim_geo, rim_hot, t_rim, lhs_rim, field, mine,
    send_q, recv_q, send_v, recv_v, row_buf, plane_buf, line_buf,
    q_send, q_recv, v_send, v_recv, s_send, s_recv,
):
    gx, gy, gz = lax.axis_index("gx"), lax.axis_index("gy"), lax.axis_index("gz")
    wide, low = gz // ZLO, gz % ZLO

    near = []
    for side in range(SIDES):
        dx, dy, dz = offset_of(side)
        near.append(((gx + (dx + NX)) % NX, (gy + (dy + NY)) % NY, (gz + (dz + NZ)) % NZ))
    plane = []
    for j in range(1, PLANE):
        dy, dw = j // ZLO, j % ZLO
        plane.append((gx, (gy + dy) % NY, ((wide + dw) % ZLO) * ZLO + low))
    line = []
    for j in range(1, LINE):
        dx, dl = j // ZLO, j % ZLO
        line.append(((gx + dx) % NX, gy, wide * ZLO + (low + dl) % ZLO))
    plane_rank = gy * ZLO + wide
    line_rank = gx * ZLO + low

    lane = lax.broadcasted_iota(jnp.int32, (8, 128), 1)
    row = lax.broadcasted_iota(jnp.int32, (8, 128), 0)

    recv_q[0:2] = jnp.zeros((2, 2, 128), F32)
    recv_q[28:32] = jnp.zeros((4, 2, 128), F32)
    for e in range(4):
        recv_v[e, 0:2] = jnp.zeros((2, 3, 128), F32)
        recv_v[e, 28:32] = jnp.zeros((4, 3, 128), F32)

    barrier = pltpu.get_barrier_semaphore()
    for where in near + plane + line:
        pl.semaphore_signal(barrier, inc=1, device_id=where, device_id_type=MESH)

    for i in range(24):
        cut = slice(128 * i, 128 * (i + 1))
        dense[0, i : i + 1, :] = own_ref[0, 0, :, cut].astype(F32)
        dense[1, i : i + 1, :] = slot_ref[0, 0, :, cut].astype(F32)
        dense[2, i : i + 1, :] = type_ref[0, 0, :, cut].astype(F32)
        for c in range(3):
            dense[3 + c, i : i + 1, :] = normal_ref[0, 0, 0, c : c + 1, cut]
        for c in range(2):
            dense[6 + c, i : i + 1, :] = radii_ref[0, 0, 0, c : c + 1, cut]

    def coefficients(kind, valid):
        out = []
        for q in range(4):
            total = jnp.zeros_like(kind)
            for t in range(TYPES):
                total = jnp.where(kind == float(t), stiff_ref[q, t], total)
            out.append(jnp.where(valid, total, 0.0))
        return [out[1], out[0] - out[1], out[2], out[3] - out[2]]

    def segments(q, v):
        low_row = dense[q, 17 + 2 * v : 18 + 2 * v, :]
        nxt = min(18 + 2 * v, 23)
        high_row = dense[q, nxt : nxt + 1, :]
        base = jnp.where(row < 4, splat(low_row), splat(high_row))
        return lanes(base, (lane % 32) + 32 * (row % 4))

    def quarter(parts):
        out = parts[3]
        for p in (2, 1, 0):
            out = jnp.where(lane < 32 * (p + 1), parts[p], out)
        return out

    kept = []
    for v in range(4):
        seg = [segments(q, v) for q in range(8)]
        side = (row + (8 * v - 2)).astype(F32)
        slot_rim = seg[1] - (GRAINS + RIM * side)
        rows = slice(8 * v, 8 * v + 8)
        send_q[rows, 0, :] = quarter([slot_rim, seg[2], seg[6], seg[7]])
        send_q[rows, 1, :] = quarter([seg[3], seg[4], seg[5], seg[5]])
        kept.append(seg)
    for v in range(4):
        for q in range(8):
            rim_geo[q, 8 * v : 8 * v + 8, :] = kept[v][q]

    pl.semaphore_wait(barrier, SIDES + PLANE - 1 + LINE - 1)

    q_copies = []
    for side in range(SIDES):
        copy = pltpu.make_async_remote_copy(
            src_ref=send_q.at[side + 2],
            dst_ref=recv_q.at[27 - side],
            send_sem=q_send.at[side],
            recv_sem=q_recv.at[25 - side],
            device_id=near[side],
            device_id_type=MESH,
        )
        copy.start()
        q_copies.append(copy)

    for v in range(3):
        rows = slice(8 * v, 8 * v + 8)
        number = (row + 8 * v) * 128 + lane
        inside = number < NEAR
        own = dense[0, rows, :]
        slot = jnp.where(inside, dense[1, rows, :], 0.0)
        idx_a[rows, :] = own.astype(jnp.int32)
        idx_b[rows, :] = slot.astype(jnp.int32)
        dense[1, rows, :] = slot
        coeff = coefficients(dense[2, rows, :], inside)
        for q in range(4):
            geo[q, rows, :] = coeff[q]

    column = lax.broadcasted_iota(jnp.int32, (128, 128), 1).astype(F32)
    pad = jnp.zeros((128 - 24, 128), F32)
    for which in range(2):
        turned = jnp.transpose(jnp.concatenate([dense[which], pad], axis=0))
        for j in range(LOCAL_ROWS):
            spread = jnp.broadcast_to(turned[:, j : j + 1], (128, 128))
            at = (which * LOCAL_ROWS + j) * 128
            for g in range(8):
                hit = jnp.where(spread == column + float(128 * g), 1.0, 0.0)
                one_hot[at : at + 128, 128 * g : 128 * (g + 1)] = hit.astype(BF16)

    t_local[...] = jnp.zeros_like(t_local)
    t_rim[...] = jnp.zeros_like(t_rim)
    lhs_local[...] = jnp.zeros_like(lhs_local)
    lhs_rim[...] = jnp.zeros_like(lhs_rim)

    def load_six(ref):
        return jnp.concatenate([ref[0, 0, 0], jnp.zeros((2, GRAINS), F32)], axis=0)

    diag = load_six(diag_ref)
    field[0] = load_six(rhs_ref)

    def split_rows(source, target, chunk, at):
        whole = source[8 * chunk : 8 * chunk + 8, :]
        high = whole.astype(BF16).astype(F32)
        rest = whole - high
        mid = rest.astype(BF16).astype(F32)
        low_part = rest - mid
        cut = slice(128 * at, 128 * (at + 1))
        target[0:16, cut] = jnp.concatenate([high, mid], axis=0).astype(BF16)
        target[16:32, cut] = jnp.concatenate([low_part, jnp.zeros_like(low_part)], axis=0).astype(BF16)

    def scatter(lhs, hot):
        out = jnp.dot(lhs[...], hot[...], preferred_element_type=F32)
        return out[0:8] + out[8:16] + out[16:24]

    def local_forces(k):
        for v in range(3):
            rows = slice(8 * v, 8 * v + 8)
            ends = []
            for index_ref in (idx_a, idx_b):
                index = index_ref[rows, :]
                fine, coarse = index % 128, index // 128
                hits = [coarse == t for t in range(1, 8)]
                got = []
                for c in range(6):
                    total = lanes(splat(field[k, c : c + 1, 0:128]), fine)
                    for t in range(1, 8):
                        table = splat(field[k, c : c + 1, 128 * t : 128 * (t + 1)])
                        total = jnp.where(hits[t - 1], lanes(table, fine), total)
                    got.append(total)
                ends.append(got)
            first, second = response(
                ends[0], ends[1],
                [dense[3 + c, rows, :] for c in range(3)],
                dense[6, rows, :], dense[7, rows, :],
                [geo[q, rows, :] for q in range(4)], True,
            )
            for c in range(6):
                t_local[pl.ds(64 * v + c, 8, stride=8), :] = first[c]
                t_local[pl.ds(192 + 64 * v + c, 8, stride=8), :] = second[c]
        for which in range(2):
            for j in range(LOCAL_ROWS):
                split_rows(t_local, lhs_local, which * 24 + j, which * LOCAL_ROWS + j)
        return scatter(lhs_local, one_hot)

    def send_values(k):
        for v in range(4):
            rows = slice(8 * v, 8 * v + 8)
            index = rim_idx[rows, :]
            fine, upper = index % 128, index >= 128
            for pair in range(3):
                got = []
                for c in (2 * pair, 2 * pair + 1):
                    halves = [lanes(splat(field[k, c : c + 1, 128 * t : 128 * (t + 1)]), fine) for t in range(2)]
                    got.append(jnp.where(upper, halves[1], halves[0]))
                both = jnp.where(lane < 64, got[0], got[1])
                swapped = jnp.where(lane % 64 < 32, pltpu.roll(both, 96, 1), pltpu.roll(both, 32, 1))
                send_v[k, rows, pair, :] = swapped
                mine[pair, rows, :] = both
        copies = []
        for side in range(SIDES):
            copy = pltpu.make_async_remote_copy(
                src_ref=send_v.at[k, side + 2],
                dst_ref=recv_v.at[k, 27 - side],
                send_sem=v_send.at[k, side],
                recv_sem=v_recv.at[k, 25 - side],
                device_id=near[side],
                device_id_type=MESH,
            )
            copy.start()
            copies.append(copy)
        return copies

    def rim_forces(k):
        for v in range(4):
            rows = slice(8 * v, 8 * v + 8)
            a, b = [], []
            for pair in range(3):
                own = mine[pair, rows, :]
                got = recv_v[k, rows, pair, :]
                a += [own, pltpu.roll(own, 64, 1)]
                b += [got, pltpu.roll(got, 64, 1)]
            first, _ = response(
                a, b,
                [rim_geo[c, rows, :] for c in range(3)],
                rim_geo[3, rows, :], rim_geo[4, rows, :],
                [rim_geo[5 + q, rows, :] for q in range(4)], False,
            )
            for c in range(6):
                t_rim[pl.ds(64 * v + c, 8, stride=8), :] = first[c]
        for i in range(SIDES):
            split_rows(t_rim, lhs_rim, i + 2, i)
        return scatter(lhs_rim, rim_hot)

    sums = []

    def total_of(x):
        folded = x[:, 0:128]
        for t in range(1, 8):
            folded = folded + x[:, 128 * t : 128 * (t + 1)]
        return jnp.sum(folded, keepdims=True)

    lane_row = lane[0:1]

    def pack(values):
        out = jnp.zeros((1, 128), F32)
        for j, value in enumerate(values):
            out = jnp.where(lane_row == j, value, out)
        return out

    def spread(stage, where, buffer, rank, value):
        row_buf[stage] = value
        buffer[rank] = value
        copies = []
        for j, device in enumerate(where):
            copy = pltpu.make_async_remote_copy(
                src_ref=row_buf.at[stage],
                dst_ref=buffer.at[rank],
                send_sem=s_send.at[stage, j],
                recv_sem=s_recv.at[stage, j],
                device_id=device,
                device_id_type=MESH,
            )
            copy.start()
            copies.append(copy)
        return copies

    def gather_sum(copies, buffer, count):
        for copy in copies:
            copy.wait_recv()
        level = [buffer[j] for j in range(count)]
        while len(level) > 1:
            level = [level[j] + level[j + 1] for j in range(0, len(level), 2)]
        return level[0]

    def lane_of(values, j):
        return jnp.sum(jnp.where(lane_row == j, values, 0.0), keepdims=True)

    for copy in q_copies:
        copy.wait_recv()
    for v in range(4):
        rows = slice(8 * v, 8 * v + 8)
        seg = [rim_geo[q, rows, :] for q in range(8)]
        got = [recv_q[rows, h, :] for h in range(2)]

        def theirs(h, p):
            return lanes(got[h], lane % 32 + 32 * p)

        ours = lane % 64 >= 32
        valid = (lane < 64) & (row + 8 * v >= 2) & (row + 8 * v < 28)
        index = jnp.where(ours, seg[0], theirs(0, 0))
        kind = jnp.where(ours, seg[2], theirs(0, 1))
        rim_idx[rows, :] = index.astype(jnp.int32)
        for c in range(3):
            rim_geo[c, rows, :] = jnp.where(ours, seg[3 + c], -theirs(1, c))
        rim_geo[3, rows, :] = jnp.where(ours, seg[6], theirs(0, 3))
        rim_geo[4, rows, :] = jnp.where(ours, seg[7], theirs(0, 2))
        coeff = coefficients(kind, valid)
        for q in range(4):
            rim_geo[5 + q, rows, :] = coeff[q]

    sent = list(q_copies)
    copies = send_values(0)
    sent += copies
    index_rows = jnp.concatenate([rim_idx[...].astype(F32), jnp.zeros((96, 128), F32)], axis=0)
    turned = jnp.transpose(index_rows)
    for i in range(SIDES):
        spread_idx = jnp.broadcast_to(turned[:, i + 2 : i + 3], (128, 128))
        for g in range(2):
            hit = jnp.where(spread_idx == column + float(128 * g), 1.0, 0.0)
            rim_hot[128 * i : 128 * (i + 1), 128 * g : 128 * (g + 1)] = hit.astype(BF16)

    def apply(k, copies):
        whole = local_forces(k)
        for copy in copies:
            copy.wait_recv()
        rim = rim_forces(k)
        forces = jnp.concatenate([whole[:, :RIM] + rim, whole[:, RIM:]], axis=1)
        return diag * field[k] - forces

    w0 = field[0]
    w1 = apply(0, copies)
    field[1] = w1
    copies = send_values(1)
    sent += copies
    early = spread(0, plane, plane_buf.at[0], plane_rank, pack([total_of(w0 * w0), total_of(w0 * w1), total_of(w1 * w1)]))
    sent += early
    w2 = apply(1, copies)
    field[2] = w2
    copies = send_values(2)
    sent += copies
    early = spread(1, line, line_buf.at[0], line_rank, gather_sum(early, plane_buf.at[0], PLANE))
    sent += early
    w3 = apply(2, copies)
    early = gather_sum(early, line_buf.at[0], LINE)
    m0, m1, m2 = lane_of(early, 0), lane_of(early, 1), lane_of(early, 2)
    inv = jnp.sqrt(m0 / m2)
    shift = m1 / m0 * inv
    inv2 = inv * inv
    u0 = w0
    w1 = w1 * inv
    w2 = w2 * inv2
    w3 = w3 * (inv2 * inv)
    u1 = w1 - shift * u0
    u2 = w2 - shift * (2.0 * w1 - shift * u0)
    u3 = w3 - shift * (3.0 * w2 - shift * (3.0 * w1 - shift * u0))
    field[3] = u3
    copies = send_values(3)
    sent += copies
    basis = [u0, u1, u2, u3]
    pairs = [(0, 0), (0, 1), (1, 1), (1, 2), (2, 2), (2, 3), (3, 3)]
    known = [total_of(basis[i] * basis[j]) for i, j in pairs]
    u4 = apply(3, copies) * inv - shift * u3
    last = total_of(u3 * u4)
    late = spread(2, plane, plane_buf.at[1], plane_rank, pack(known + [last]))
    sent += late
    late = spread(3, line, line_buf.at[1], line_rank, gather_sum(late, plane_buf.at[1], PLANE))
    sent += late
    sums = gather_sum(late, line_buf.at[1], LINE)
    mu = [lane_of(sums, j) for j in range(8)]

    scale = 1.0 / inv

    def inner(p, q):
        by_degree = {}
        for i, x in enumerate(p):
            for j, y in enumerate(q):
                term = x * y
                by_degree[i + j] = by_degree[i + j] + term if i + j in by_degree else term
        out = None
        for degree, term in by_degree.items():
            term = term * mu[degree]
            out = term if out is None else out + term
        return out

    one = jnp.ones((1, 1), F32)
    res, direction, answer = [one], [one], []
    norm = mu[0]
    for step in range(4):
        image = [shift * direction[0]]
        for i in range(1, len(direction)):
            image.append(direction[i - 1] + shift * direction[i])
        image.append(direction[-1])
        image = [scale * value for value in image]
        alpha = norm / inner(direction, image)
        answer = [
            alpha * direction[i] + (answer[i] if i < len(answer) else 0.0)
            for i in range(len(direction))
        ]
        res = [
            (res[i] if i < len(res) else 0.0) - alpha * image[i]
            for i in range(len(image))
        ]
        if step < 3:
            fresh = inner(res, res)
            ratio = fresh / norm
            direction = [
                res[i] + (ratio * direction[i] if i < len(direction) else 0.0)
                for i in range(len(res))
            ]
            norm = fresh
    basis.append(u4)
    x = answer[0] * basis[0]
    for i in range(1, 4):
        x = x + answer[i] * basis[i]
    r = res[0] * basis[0]
    for i in range(1, 5):
        r = r + res[i] * basis[i]
    x_ref[0, 0, 0] = x[0:6]
    r_ref[0, 0, 0] = r[0:6]
    for copy in sent:
        copy.wait_send()


def shards(*arguments):
    vmem = pl.BlockSpec(memory_space=pltpu.VMEM)
    smem = pl.BlockSpec(memory_space=pltpu.SMEM)
    out = jax.ShapeDtypeStruct((1, 1, 1, 6, GRAINS), F32)
    dma = pltpu.SemaphoreType.DMA
    return pl.pallas_call(
        kernel,
        out_shape=(out, out),
        in_specs=[vmem, vmem, smem] + [vmem] * 5,
        out_specs=(vmem, vmem),
        scratch_shapes=[
            pltpu.VMEM((8, 24, 128), F32),
            pltpu.VMEM((24, 128), jnp.int32),
            pltpu.VMEM((24, 128), jnp.int32),
            pltpu.VMEM((4, 24, 128), F32),
            pltpu.VMEM((2 * LOCAL_ROWS * 128, GRAINS), BF16),
            pltpu.VMEM((2 * 24 * 8, 128), F32),
            pltpu.VMEM((32, 2 * LOCAL_ROWS * 128), BF16),
            pltpu.VMEM((32, 128), jnp.int32),
            pltpu.VMEM((9, 32, 128), F32),
            pltpu.VMEM((SIDES * 128, RIM), BF16),
            pltpu.VMEM((32 * 8, 128), F32),
            pltpu.VMEM((32, SIDES * 128), BF16),
            pltpu.VMEM((4, 8, GRAINS), F32),
            pltpu.VMEM((3, 32, 128), F32),
            pltpu.VMEM((32, 2, 128), F32),
            pltpu.VMEM((32, 2, 128), F32),
            pltpu.VMEM((4, 32, 3, 128), F32),
            pltpu.VMEM((4, 32, 3, 128), F32),
            pltpu.VMEM((4, 1, 128), F32),
            pltpu.VMEM((2, PLANE, 1, 128), F32),
            pltpu.VMEM((2, LINE, 1, 128), F32),
            dma((SIDES,)),
            dma((SIDES,)),
            dma((4, SIDES)),
            dma((4, SIDES)),
            dma((4, PLANE)),
            dma((4, PLANE)),
        ],
        compiler_params=pltpu.CompilerParams(
            collective_id=0, has_side_effects=True, vmem_limit_bytes=56 * 1024 * 1024
        ),
    )(*arguments)


def solution(mesh):
    placed = P("gx", "gy", "gz", None, None)
    flat = P("gx", "gy", "gz", None)
    return jax.shard_map(
        shards,
        mesh=mesh,
        in_specs=(placed, placed, P(), flat, flat, flat, placed, placed),
        out_specs=(placed, placed),
        check_vma=False,
    )
```

time: 712 us -> 82.1 us (0.12); the launches traced: 701 us -> 81.8 us
  blocking collectives: 184 us -> 0 us
  other arithmetic: 180 us -> 0 us
  local copies, waits for them, and re-layouts: 176 us -> 4.79 us
  starting transfers between devices: 132 us -> 0 us
  Pallas kernels: 0 us -> 76.3 us
  between operations: 16.5 us -> 0.66 us
  waiting for transfers between devices: 12.4 us -> 0 us
    psum x20 -> x0, blocking collectives: 184 us -> none  [one_axis_at_a_time(): value = lax.psum(value, axis)]
    scatter-add x12 -> x0, other arithmetic: 168 us -> none  [the longest x4 74.2 us: operate(): forces.at[:, near_grain].add(jnp.where(far_slot[None], 0.0, on_second))]
    gather x42 -> x0, local copies, waits for them, and re-layouts: 140 us -> none  [the longest x8 42.3 us: operate(): rim_flat[:, ghost_column]]
    ppermute x36 -> x0, starting transfers between devices: 132 us -> none  [the longest x18 89.2 us: with_halo(): lax.ppermute(lax.slice_in_dim(block, 0, width, axis=dim), axis, backward)]
    pallas_call x0 -> x1, Pallas kernels: none -> 76.3 us  [shards(): pl.pallas_call(kernel, out_shape=(out, out), in_specs=[vmem, vmem, smem]...]
    reshape x9 -> x0, local copies, waits for them, and re-layouts: 17.3 us -> none  [the longest x4 9.71 us: operate(): rim_flat = jnp.moveaxis(rims.reshape(27, 6, rim), 1, 0).reshape(6, 27 * rim)]
    ppermute x36 -> x0, waiting for transfers between devices: 12.4 us -> none  [the longest x18 9.19 us: with_halo(): lax.ppermute(lax.slice_in_dim(block, 0, width, axis=dim), axis, backward)]
  transfers between devices with their start and end apart: 36 -> 0, of which waited for: 4 -> 0; matrix products, arithmetic and copies ran while one was open for 21% -> 0% of each run, Pallas kernels for 0% -> 0%
where the time goes in v1:
time: 82.1 us; the launch traced here: 81.8 us
  Pallas kernels  76.3 us (93%)
  local copies, waits for them, and re-layouts  4.79 us (6%)
    pallas_call x1, Pallas kernels, shards(): pl.pallas_call(kernel, out_shape=(out, out), in_specs=[vmem, vmem, smem]...  76.3 us
    unnamed x9, local copies, waits for them, and re-layouts  2.76 us
    pallas_call x2, local copies, waits for them, and re-layouts, shards(): pl.pallas_call(kernel, out_shape=(out, out), in_specs=[vmem, vmem, smem]...  2.03 us

profile of v1, /device:TPU:1, one launch (start us, length us, event | category | flops | bytes accessed | tf_op | source)
XLA Modules:
  0.0 81.8 jit_solution(11511778184638128430)
XLA Ops:
  0.6 0.0 copy-start.2
  0.6 1.4 %copy.10.rhs_ref = f32[1,1,1,6,1024]{4,3,2,1,0:T(8,128)} copy(f32[1,1,1,6,1024]{4,2,3,1,0:T(1,128)} %param.8) | data formatting | bytes 49152 | tf_op args[0]
  2.0 0.0 copy-done.2
  2.0 0.0 copy-start
  2.0 0.6 copy.11.diag_ref
  2.6 0.2 copy-done
  2.8 0.6 copy.12.normal_ref
  3.4 76.3 %shard_map.95 = (f32[1,1,1,6,1024]{4,3,2,1,0:T(8,128)}, f32[1,1,1,6,1024]{4,3,2,1,0:T(8,128)}) custom-call(f32[1,1,1,6,1024]{4,3,2,1,0:T(8,128)} %copy.10.rhs_ref, f32[1,1,1,6,1024]{4,3,2,1,0:T(8,128)} %copy.11.diag_ref, f32[4,4]{1,0:T(4,128)} %stiff_ref.1, s32[1,1,1,3072]{3,2,1,0:T(1,128)} %own_ref.1, s32[1,1,1,3072]{3,2,1,0:T(1,128)} %slot_ref.1, ...), custom_call_target="tpu_custom_call" | custom-call | tf_op jit(solution)/shard_map/pallas_call | solution.py:476
  79.7 0.0 copy-start.1
  79.7 1.4 %copy.13 = f32[1,1,1,6,1024]{4,2,3,1,0:T(1,128)} copy(f32[1,1,1,6,1024]{4,3,2,1,0:T(8,128)} %get-tuple-element.2) | data formatting | bytes 49152 | tf_op jit(solution)/shard_map/pallas_call | solution.py:476
  81.1 0.0 copy-done.1
  81.1 0.6 copy.14
Async XLA Ops:
  0.6 1.4 %copy-start.2 = (f32[1,1,1,6,1024]{4,2,3,1,0:T(1,128)S(1)}, f32[1,1,1,6,1024]{4,2,3,1,0:T(1,128)}, u32[]{:S(2)}) copy-start(f32[1,1,1,6,1024]{4,2,3,1,0:T(1,128)} %param.9) | copy-start | bytes 73732
  2.0 0.8 copy-start
  79.7 1.4 %copy-start.1 = (f32[1,1,1,6,1024]{4,3,2,1,0:T(8,128)S(1)}, f32[1,1,1,6,1024]{4,3,2,1,0:T(8,128)}, u32[]{:S(2)}) copy-start(f32[1,1,1,6,1024]{4,3,2,1,0:T(8,128)} %get-tuple-element.3) | copy-start | bytes 73732

commit v2 on v1

--- a/solution.py
+++ b/solution.py
@@ -63,9 +63,9 @@
 
 def kernel(
     rhs_ref, diag_ref, stiff_ref, own_ref, slot_ref, type_ref, normal_ref, radii_ref,
-    x_ref, r_ref,
+    x_ref,
     dense, idx_a, idx_b, geo, one_hot, t_local, lhs_local,
-    rim_idx, rim_geo, rim_hot, t_rim, lhs_rim, field, mine,
+    rim_idx, rim_far, rim_geo, rim_hot, t_rim, lhs_rim, field, forces, mine,
     send_q, recv_q, send_v, recv_v, row_buf, plane_buf, line_buf,
     q_send, q_recv, v_send, v_recv, s_send, s_recv,
 ):
@@ -90,9 +90,9 @@
     lane = lax.broadcasted_iota(jnp.int32, (8, 128), 1)
     row = lax.broadcasted_iota(jnp.int32, (8, 128), 0)
 
-    recv_q[0:2] = jnp.zeros((2, 2, 128), F32)
-    recv_q[28:32] = jnp.zeros((4, 2, 128), F32)
-    for e in range(4):
+    recv_q[0:2] = jnp.zeros((2, 14, 128), F32)
+    recv_q[28:32] = jnp.zeros((4, 14, 128), F32)
+    for e in range(3):
         recv_v[e, 0:2] = jnp.zeros((2, 3, 128), F32)
         recv_v[e, 28:32] = jnp.zeros((4, 3, 128), F32)
 
@@ -100,15 +100,14 @@
     for where in near + plane + line:
         pl.semaphore_signal(barrier, inc=1, device_id=where, device_id_type=MESH)
 
-    for i in range(24):
-        cut = slice(128 * i, 128 * (i + 1))
-        dense[0, i : i + 1, :] = own_ref[0, 0, :, cut].astype(F32)
-        dense[1, i : i + 1, :] = slot_ref[0, 0, :, cut].astype(F32)
-        dense[2, i : i + 1, :] = type_ref[0, 0, :, cut].astype(F32)
-        for c in range(3):
-            dense[3 + c, i : i + 1, :] = normal_ref[0, 0, 0, c : c + 1, cut]
-        for c in range(2):
-            dense[6 + c, i : i + 1, :] = radii_ref[0, 0, 0, c : c + 1, cut]
+    dense[0] = own_ref[...].astype(F32)
+    dense[1] = slot_ref[...].astype(F32)
+    dense[2] = type_ref[...].astype(F32)
+    for c in range(3):
+        dense[3 + c] = normal_ref[24 * c : 24 * c + 24, :]
+    for c in range(2):
+        for i in range(24):
+            dense[6 + c, i : i + 1, :] = radii_ref[0, 0, 0, c : c + 1, 128 * i : 128 * (i + 1)]
 
     def coefficients(kind, valid):
         out = []
@@ -138,12 +137,16 @@
         side = (row + (8 * v - 2)).astype(F32)
         slot_rim = seg[1] - (GRAINS + RIM * side)
         rows = slice(8 * v, 8 * v + 8)
-        send_q[rows, 0, :] = quarter([slot_rim, seg[2], seg[6], seg[7]])
-        send_q[rows, 1, :] = quarter([seg[3], seg[4], seg[5], seg[5]])
+        send_q[rows, 12, :] = quarter([slot_rim, seg[2], seg[6], seg[7]])
+        send_q[rows, 13, :] = quarter([seg[3], seg[4], seg[5], seg[0]])
+        seg[1] = slot_rim
         kept.append(seg)
     for v in range(4):
         for q in range(8):
             rim_geo[q, 8 * v : 8 * v + 8, :] = kept[v][q]
+    rim = jnp.concatenate([rhs_ref[8 * c : 8 * c + 2, :] for c in range(6)], axis=0)
+    for side in range(SIDES):
+        send_q[side + 2, 0:12, :] = rim
 
     pl.semaphore_wait(barrier, SIDES + PLANE - 1 + LINE - 1)
 
@@ -184,19 +187,26 @@
                 hit = jnp.where(spread == column + float(128 * g), 1.0, 0.0)
                 one_hot[at : at + 128, 128 * g : 128 * (g + 1)] = hit.astype(BF16)
 
+    def rim_rows(turned, first_row, at):
+        for i in range(SIDES):
+            spread_idx = jnp.broadcast_to(turned[first_row : first_row + 32, i + 2 : i + 3], (32, 128))
+            start = 64 * i + at
+            for g in range(2):
+                hit = jnp.where(spread_idx == column[0:32] + float(128 * g), 1.0, 0.0)
+                rim_hot[start : start + 32, 128 * g : 128 * (g + 1)] = hit.astype(BF16)
+
+    rim_pad = jnp.zeros((96, 128), F32)
+    rim_rows(jnp.transpose(jnp.concatenate([rim_geo[0], rim_pad], axis=0)), 0, 32)
+
     t_local[...] = jnp.zeros_like(t_local)
     t_rim[...] = jnp.zeros_like(t_rim)
     lhs_local[...] = jnp.zeros_like(lhs_local)
     lhs_rim[...] = jnp.zeros_like(lhs_rim)
 
-    def load_six(ref):
-        return jnp.concatenate([ref[0, 0, 0], jnp.zeros((2, GRAINS), F32)], axis=0)
-
-    diag = load_six(diag_ref)
-    field[0] = load_six(rhs_ref)
-
-    def split_rows(source, target, chunk, at):
-        whole = source[8 * chunk : 8 * chunk + 8, :]
+    diag = diag_ref[...]
+    field[0] = rhs_ref[...]
+
+    def split_rows(whole, target, at):
         high = whole.astype(BF16).astype(F32)
         rest = whole - high
         mid = rest.astype(BF16).astype(F32)
@@ -219,9 +229,9 @@
                 hits = [coarse == t for t in range(1, 8)]
                 got = []
                 for c in range(6):
-                    total = lanes(splat(field[k, c : c + 1, 0:128]), fine)
+                    total = lanes(splat(field[k, 8 * c : 8 * c + 1, :]), fine)
                     for t in range(1, 8):
-                        table = splat(field[k, c : c + 1, 128 * t : 128 * (t + 1)])
+                        table = splat(field[k, 8 * c + t : 8 * c + t + 1, :])
                         total = jnp.where(hits[t - 1], lanes(table, fine), total)
                     got.append(total)
                 ends.append(got)
@@ -236,10 +246,11 @@
                 t_local[pl.ds(192 + 64 * v + c, 8, stride=8), :] = second[c]
         for which in range(2):
             for j in range(LOCAL_ROWS):
-                split_rows(t_local, lhs_local, which * 24 + j, which * LOCAL_ROWS + j)
+                start = 8 * (which * 24 + j)
+                split_rows(t_local[start : start + 8, :], lhs_local, which * LOCAL_ROWS + j)
         return scatter(lhs_local, one_hot)
 
-    def send_values(k):
+    def own_values(k, send):
         for v in range(4):
             rows = slice(8 * v, 8 * v + 8)
             index = rim_idx[rows, :]
@@ -247,19 +258,23 @@
             for pair in range(3):
                 got = []
                 for c in (2 * pair, 2 * pair + 1):
-                    halves = [lanes(splat(field[k, c : c + 1, 128 * t : 128 * (t + 1)]), fine) for t in range(2)]
+                    halves = [lanes(splat(field[k, 8 * c + t : 8 * c + t + 1, :]), fine) for t in range(2)]
                     got.append(jnp.where(upper, halves[1], halves[0]))
                 both = jnp.where(lane < 64, got[0], got[1])
-                swapped = jnp.where(lane % 64 < 32, pltpu.roll(both, 96, 1), pltpu.roll(both, 32, 1))
-                send_v[k, rows, pair, :] = swapped
                 mine[pair, rows, :] = both
+                if send:
+                    swapped = jnp.where(lane % 64 < 32, pltpu.roll(both, 96, 1), pltpu.roll(both, 32, 1))
+                    send_v[k - 1, rows, pair, :] = swapped
+
+    def send_values(k):
+        own_values(k, True)
         copies = []
         for side in range(SIDES):
             copy = pltpu.make_async_remote_copy(
-                src_ref=send_v.at[k, side + 2],
-                dst_ref=recv_v.at[k, 27 - side],
-                send_sem=v_send.at[k, side],
-                recv_sem=v_recv.at[k, 25 - side],
+                src_ref=send_v.at[k - 1, side + 2],
+                dst_ref=recv_v.at[k - 1, 27 - side],
+                send_sem=v_send.at[k - 1, side],
+                recv_sem=v_recv.at[k - 1, 25 - side],
                 device_id=near[side],
                 device_id_type=MESH,
             )
@@ -273,9 +288,15 @@
             a, b = [], []
             for pair in range(3):
                 own = mine[pair, rows, :]
-                got = recv_v[k, rows, pair, :]
                 a += [own, pltpu.roll(own, 64, 1)]
-                b += [got, pltpu.roll(got, 64, 1)]
+                if k > 0:
+                    got = recv_v[k - 1, rows, pair, :]
+                    b += [got, pltpu.roll(got, 64, 1)]
+                else:
+                    far = rim_far[rows, :]
+                    for c in (2 * pair, 2 * pair + 1):
+                        halves = [lanes(recv_q[rows, 2 * c + t, :], far % 128) for t in range(2)]
+                        b.append(jnp.where(far >= 128, halves[1], halves[0]))
             first, _ = response(
                 a, b,
                 [rim_geo[c, rows, :] for c in range(3)],
@@ -284,16 +305,18 @@
             )
             for c in range(6):
                 t_rim[pl.ds(64 * v + c, 8, stride=8), :] = first[c]
-        for i in range(SIDES):
-            split_rows(t_rim, lhs_rim, i + 2, i)
+        for i in range(SIDES // 2):
+            start = 16 * (i + 1)
+            even, odd = t_rim[start : start + 8, :], t_rim[start + 8 : start + 16, :]
+            split_rows(jnp.where(lane < 64, even, pltpu.roll(odd, 64, 1)), lhs_rim, i)
         return scatter(lhs_rim, rim_hot)
 
     sums = []
 
     def total_of(x):
-        folded = x[:, 0:128]
-        for t in range(1, 8):
-            folded = folded + x[:, 128 * t : 128 * (t + 1)]
+        folded = x[0:8]
+        for t in range(1, 6):
+            folded = folded + x[8 * t : 8 * t + 8]
         return jnp.sum(folded, keepdims=True)
 
     lane_row = lane[0:1]
@@ -332,50 +355,50 @@
     def lane_of(values, j):
         return jnp.sum(jnp.where(lane_row == j, values, 0.0), keepdims=True)
 
-    for copy in q_copies:
-        copy.wait_recv()
-    for v in range(4):
-        rows = slice(8 * v, 8 * v + 8)
-        seg = [rim_geo[q, rows, :] for q in range(8)]
-        got = [recv_q[rows, h, :] for h in range(2)]
-
-        def theirs(h, p):
-            return lanes(got[h], lane % 32 + 32 * p)
-
-        ours = lane % 64 >= 32
-        valid = (lane < 64) & (row + 8 * v >= 2) & (row + 8 * v < 28)
-        index = jnp.where(ours, seg[0], theirs(0, 0))
-        kind = jnp.where(ours, seg[2], theirs(0, 1))
-        rim_idx[rows, :] = index.astype(jnp.int32)
-        for c in range(3):
-            rim_geo[c, rows, :] = jnp.where(ours, seg[3 + c], -theirs(1, c))
-        rim_geo[3, rows, :] = jnp.where(ours, seg[6], theirs(0, 3))
-        rim_geo[4, rows, :] = jnp.where(ours, seg[7], theirs(0, 2))
-        coeff = coefficients(kind, valid)
-        for q in range(4):
-            rim_geo[5 + q, rows, :] = coeff[q]
+    def meet():
+        for v in range(4):
+            rows = slice(8 * v, 8 * v + 8)
+            seg = [rim_geo[q, rows, :] for q in range(8)]
+            got = [recv_q[rows, 12 + h, :] for h in range(2)]
+
+            def theirs(h, p):
+                return lanes(got[h], lane % 32 + 32 * p)
+
+            ours = lane % 64 >= 32
+            valid = (lane < 64) & (row + 8 * v >= 2) & (row + 8 * v < 28)
+            index = jnp.where(ours, seg[0], theirs(0, 0))
+            kind = jnp.where(ours, seg[2], theirs(0, 1))
+            rim_idx[rows, :] = index.astype(jnp.int32)
+            rim_far[rows, :] = jnp.where(ours, seg[1], theirs(1, 3)).astype(jnp.int32)
+            for c in range(3):
+                rim_geo[c, rows, :] = jnp.where(ours, seg[3 + c], -theirs(1, c))
+            rim_geo[3, rows, :] = jnp.where(ours, seg[6], theirs(0, 3))
+            rim_geo[4, rows, :] = jnp.where(ours, seg[7], theirs(0, 2))
+            coeff = coefficients(kind, valid)
+            for q in range(4):
+                rim_geo[5 + q, rows, :] = coeff[q]
+        own_values(0, False)
+        turned = jnp.transpose(jnp.concatenate([rim_idx[...].astype(F32), rim_pad], axis=0))
+        rim_rows(turned, 0, 0)
 
     sent = list(q_copies)
-    copies = send_values(0)
-    sent += copies
-    index_rows = jnp.concatenate([rim_idx[...].astype(F32), jnp.zeros((96, 128), F32)], axis=0)
-    turned = jnp.transpose(index_rows)
-    for i in range(SIDES):
-        spread_idx = jnp.broadcast_to(turned[:, i + 2 : i + 3], (128, 128))
-        for g in range(2):
-            hit = jnp.where(spread_idx == column + float(128 * g), 1.0, 0.0)
-            rim_hot[128 * i : 128 * (i + 1), 128 * g : 128 * (g + 1)] = hit.astype(BF16)
 
     def apply(k, copies):
         whole = local_forces(k)
         for copy in copies:
             copy.wait_recv()
+        if k == 0:
+            meet()
         rim = rim_forces(k)
-        forces = jnp.concatenate([whole[:, :RIM] + rim, whole[:, RIM:]], axis=1)
-        return diag * field[k] - forces
+        for t in range(8):
+            part = whole[:, 128 * t : 128 * (t + 1)]
+            if t < 2:
+                part = part + rim[:, 128 * t : 128 * (t + 1)]
+            forces[pl.ds(t, 8, stride=8), :] = part
+        return diag * field[k] - forces[0:48, :]
 
     w0 = field[0]
-    w1 = apply(0, copies)
+    w1 = apply(0, q_copies)
     field[1] = w1
     copies = send_values(1)
     sent += copies
@@ -462,22 +485,25 @@
     r = res[0] * basis[0]
     for i in range(1, 5):
         r = r + res[i] * basis[i]
-    x_ref[0, 0, 0] = x[0:6]
-    r_ref[0, 0, 0] = r[0:6]
+    x_ref[0:48] = x
+    x_ref[48:96] = r
     for copy in sent:
         copy.wait_send()
 
 
 def shards(*arguments):
+    arguments = [
+        x if x.ndim == 2 or x.shape[3] == 2 else x.reshape(x.size // 128, 128) for x in arguments
+    ]
     vmem = pl.BlockSpec(memory_space=pltpu.VMEM)
     smem = pl.BlockSpec(memory_space=pltpu.SMEM)
-    out = jax.ShapeDtypeStruct((1, 1, 1, 6, GRAINS), F32)
+    out = jax.ShapeDtypeStruct((48, 128), F32)
     dma = pltpu.SemaphoreType.DMA
-    return pl.pallas_call(
+    outs = pl.pallas_call(
         kernel,
-        out_shape=(out, out),
+        out_shape=jax.ShapeDtypeStruct((96,128),F32),
         in_specs=[vmem, vmem, smem] + [vmem] * 5,
-        out_specs=(vmem, vmem),
+        out_specs=vmem,
         scratch_shapes=[
             pltpu.VMEM((8, 24, 128), F32),
             pltpu.VMEM((24, 128), jnp.int32),
@@ -487,23 +513,25 @@
             pltpu.VMEM((2 * 24 * 8, 128), F32),
             pltpu.VMEM((32, 2 * LOCAL_ROWS * 128), BF16),
             pltpu.VMEM((32, 128), jnp.int32),
+            pltpu.VMEM((32, 128), jnp.int32),
             pltpu.VMEM((9, 32, 128), F32),
-            pltpu.VMEM((SIDES * 128, RIM), BF16),
+            pltpu.VMEM((SIDES * 64, RIM), BF16),
             pltpu.VMEM((32 * 8, 128), F32),
-            pltpu.VMEM((32, SIDES * 128), BF16),
-            pltpu.VMEM((4, 8, GRAINS), F32),
+            pltpu.VMEM((32, SIDES * 64), BF16),
+            pltpu.VMEM((4, 48, 128), F32),
+            pltpu.VMEM((64, 128), F32),
             pltpu.VMEM((3, 32, 128), F32),
-            pltpu.VMEM((32, 2, 128), F32),
-            pltpu.VMEM((32, 2, 128), F32),
-            pltpu.VMEM((4, 32, 3, 128), F32),
-            pltpu.VMEM((4, 32, 3, 128), F32),
+            pltpu.VMEM((32, 14, 128), F32),
+            pltpu.VMEM((32, 14, 128), F32),
+            pltpu.VMEM((3, 32, 3, 128), F32),
+            pltpu.VMEM((3, 32, 3, 128), F32),
             pltpu.VMEM((4, 1, 128), F32),
             pltpu.VMEM((2, PLANE, 1, 128), F32),
             pltpu.VMEM((2, LINE, 1, 128), F32),
             dma((SIDES,)),
             dma((SIDES,)),
-            dma((4, SIDES)),
-            dma((4, SIDES)),
+            dma((3, SIDES)),
+            dma((3, SIDES)),
             dma((4, PLANE)),
             dma((4, PLANE)),
         ],
@@ -511,6 +539,7 @@
             collective_id=0, has_side_effects=True, vmem_limit_bytes=56 * 1024 * 1024
         ),
     )(*arguments)
+    return tuple(outs[48*i:48*i+48].reshape(1, 1, 1, 6, GRAINS) for i in range(2))
 
 
 def solution(mesh):

time: 82.1 us -> 73.5 us (0.90)
  Pallas kernels: 76.3 us -> 71.2 us
  local copies, waits for them, and re-layouts: 4.79 us -> 1.38 us
    pallas_call x1, Pallas kernels: 76.3 us -> 71.2 us  [shards(): pl.pallas_call(kernel, out_shape=jax.ShapeDtypeStruct((96, 128), F32), in...]
    unnamed x9 -> x0, local copies, waits for them, and re-layouts: 2.76 us -> none
    pallas_call x2 -> x0, local copies, waits for them, and re-layouts: 2.03 us -> none  [shards(): pl.pallas_call(kernel, out_shape=(out, out), in_specs=[vmem, vmem, smem]...]
    slice x0 -> x1, local copies, waits for them, and re-layouts: none -> 1.38 us  [shards(): outs[48 * i:48 * i + 48].reshape(1, 1, 1, 6, GRAINS)]
where the time goes in v2:
time: 73.5 us; the launch traced here: 73.2 us
  Pallas kernels  71.2 us (97%)
  local copies, waits for them, and re-layouts  1.38 us (2%)
    pallas_call x1, Pallas kernels, shards(): pl.pallas_call(kernel, out_shape=jax.ShapeDtypeStruct((96, 128), F32), in...  71.2 us

profile of v2, /device:TPU:1, one launch (start us, length us, event | category | flops | bytes accessed | tf_op | source)
XLA Modules:
  0.0 73.2 jit_solution(16218777230368105483)
XLA Ops:
  0.6 71.2 %shard_map.95 = f32[96,128]{1,0:T(8,128)} custom-call(f32[48,128]{1,0:T(8,128)} %bitcast.9, f32[48,128]{1,0:T(8,128)} %bitcast.10, f32[4,4]{1,0:T(4,128)} %stiff_ref.1, s32[24,128]{1,0:T(8,128)} %bitcast.13, s32[24,128]{1,0:T(8,128)} %bitcast.14, s32[24,128]{1,0:T(8,128)} %bitcast.15, f32[72,128]{1,0:T(8,128)} %bitcast.8, f32[1,1,1,2,3072]{4,3,2,1,0:T(2,128)} %radii_ref.1), custom_call_target="tpu_custom_call" | custom-call | tf_op jit(solution)/shard_map/pallas_call | solution.py:502
  71.8 1.4 %fusion = (f32[48,128]{1,0:T(8,128)}, f32[48,128]{1,0:T(8,128)}) fusion(f32[96,128]{1,0:T(8,128)} %shard_map.95), kind=kLoop, calls=%fused_computation | loop fusion | bytes 98304 | tf_op jit(solution)/shard_map/slice | solution.py:542

commit v3 on v2

--- a/solution.py
+++ b/solution.py
@@ -48,7 +48,8 @@
     lever = cross(n, force)
     first = force + [ra * lever[c] + moment[c] for c in range(3)]
     if not both:
-        return first, None
+        work = [force[c] * delta[c] + moment[c] * theta[c] for c in range(3)]
+        return first, work[0] + work[1] + work[2]
     second = [-f for f in force] + [rb * lever[c] - moment[c] for c in range(3)]
     return first, second
 
@@ -62,16 +63,31 @@
 
 
 def kernel(
+    rhs_in, diag_in, stiff_in, own_in, slot_in, type_in, normal_in, radii_in,
+    x_ref,
     rhs_ref, diag_ref, stiff_ref, own_ref, slot_ref, type_ref, normal_ref, radii_ref,
-    x_ref,
     dense, idx_a, idx_b, geo, one_hot, t_local, lhs_local,
-    rim_idx, rim_far, rim_geo, rim_hot, t_rim, lhs_rim, field, forces, mine,
+    rim_idx, rim_far, rim_out, rim_geo, rim_hot, t_rim, lhs_rim, field, diag, mine,
     send_q, recv_q, send_v, recv_v, row_buf, plane_buf, line_buf,
-    q_send, q_recv, v_send, v_recv, s_send, s_recv,
+    in_sem, q_send, q_recv, v_send, v_recv, s_send, s_recv,
 ):
+    loads = []
+    for j, (source, target) in enumerate((
+        (rhs_in, rhs_ref), (own_in, own_ref), (slot_in, slot_ref), (type_in, type_ref),
+        (normal_in, normal_ref), (radii_in.at[0, 0, 0], radii_ref), (stiff_in, stiff_ref),
+        (diag_in, diag_ref),
+    )):
+        load = pltpu.make_async_copy(source, target, in_sem.at[j])
+        load.start()
+        loads.append(load)
     gx, gy, gz = lax.axis_index("gx"), lax.axis_index("gy"), lax.axis_index("gz")
     wide, low = gz // ZLO, gz % ZLO
 
+    def distance(side):
+        dx, dy, dz = offset_of(side)
+        return (dx == 0, dx * dz >= 0, -abs(dz), -abs(dy))
+
+    farthest_first = sorted(range(SIDES), key=distance)
     near = []
     for side in range(SIDES):
         dx, dy, dz = offset_of(side)
@@ -90,15 +106,18 @@
     lane = lax.broadcasted_iota(jnp.int32, (8, 128), 1)
     row = lax.broadcasted_iota(jnp.int32, (8, 128), 0)
 
+    barrier = pltpu.get_barrier_semaphore()
+    for where in near + plane + line:
+        pl.semaphore_signal(barrier, inc=1, device_id=where, device_id_type=MESH)
+
     recv_q[0:2] = jnp.zeros((2, 14, 128), F32)
     recv_q[28:32] = jnp.zeros((4, 14, 128), F32)
     for e in range(3):
         recv_v[e, 0:2] = jnp.zeros((2, 3, 128), F32)
         recv_v[e, 28:32] = jnp.zeros((4, 3, 128), F32)
 
-    barrier = pltpu.get_barrier_semaphore()
-    for where in near + plane + line:
-        pl.semaphore_signal(barrier, inc=1, device_id=where, device_id_type=MESH)
+    for load in loads:
+        load.wait()
 
     dense[0] = own_ref[...].astype(F32)
     dense[1] = slot_ref[...].astype(F32)
@@ -107,14 +126,19 @@
         dense[3 + c] = normal_ref[24 * c : 24 * c + 24, :]
     for c in range(2):
         for i in range(24):
-            dense[6 + c, i : i + 1, :] = radii_ref[0, 0, 0, c : c + 1, 128 * i : 128 * (i + 1)]
+            dense[6 + c, i : i + 1, :] = radii_ref[c : c + 1, 128 * i : 128 * (i + 1)]
+
+    stiffness = [
+        [jnp.broadcast_to(stiff_ref[q : q + 1, t : t + 1], (8, 128)) for t in range(TYPES)]
+        for q in range(4)
+    ]
 
     def coefficients(kind, valid):
         out = []
         for q in range(4):
             total = jnp.zeros_like(kind)
             for t in range(TYPES):
-                total = jnp.where(kind == float(t), stiff_ref[q, t], total)
+                total = jnp.where(kind == float(t), stiffness[q][t], total)
             out.append(jnp.where(valid, total, 0.0))
         return [out[1], out[0] - out[1], out[2], out[3] - out[2]]
 
@@ -151,7 +175,7 @@
     pl.semaphore_wait(barrier, SIDES + PLANE - 1 + LINE - 1)
 
     q_copies = []
-    for side in range(SIDES):
+    for side in farthest_first:
         copy = pltpu.make_async_remote_copy(
             src_ref=send_q.at[side + 2],
             dst_ref=recv_q.at[27 - side],
@@ -203,8 +227,10 @@
     lhs_local[...] = jnp.zeros_like(lhs_local)
     lhs_rim[...] = jnp.zeros_like(lhs_rim)
 
-    diag = diag_ref[...]
-    field[0] = rhs_ref[...]
+    field[0, 0:48, :] = rhs_ref[...]
+    field[0, 48:64, :] = jnp.zeros((16, 128), F32)
+    diag[0:48, :] = diag_ref[...]
+    diag[48:64, :] = jnp.zeros((16, 128), F32)
 
     def split_rows(whole, target, at):
         high = whole.astype(BF16).astype(F32)
@@ -250,26 +276,31 @@
                 split_rows(t_local[start : start + 8, :], lhs_local, which * LOCAL_ROWS + j)
         return scatter(lhs_local, one_hot)
 
-    def own_values(k, send):
+    def rim_values(k, index_ref, v):
+        index = index_ref[8 * v : 8 * v + 8, :]
+        fine, upper = index % 128, index >= 128
+        out = []
+        for pair in range(3):
+            got = []
+            for c in (2 * pair, 2 * pair + 1):
+                halves = [lanes(splat(field[k, 8 * c + t : 8 * c + t + 1, :]), fine) for t in range(2)]
+                got.append(jnp.where(upper, halves[1], halves[0]))
+            out.append(jnp.where(lane < 64, got[0], got[1]))
+        return out
+
+    def own_values(k):
         for v in range(4):
-            rows = slice(8 * v, 8 * v + 8)
-            index = rim_idx[rows, :]
-            fine, upper = index % 128, index >= 128
+            got = rim_values(k, rim_idx, v)
             for pair in range(3):
-                got = []
-                for c in (2 * pair, 2 * pair + 1):
-                    halves = [lanes(splat(field[k, 8 * c + t : 8 * c + t + 1, :]), fine) for t in range(2)]
-                    got.append(jnp.where(upper, halves[1], halves[0]))
-                both = jnp.where(lane < 64, got[0], got[1])
-                mine[pair, rows, :] = both
-                if send:
-                    swapped = jnp.where(lane % 64 < 32, pltpu.roll(both, 96, 1), pltpu.roll(both, 32, 1))
-                    send_v[k - 1, rows, pair, :] = swapped
+                mine[pair, 8 * v : 8 * v + 8, :] = got[pair]
 
     def send_values(k):
-        own_values(k, True)
+        for v in range(4):
+            got = rim_values(k, rim_out, v)
+            for pair in range(3):
+                send_v[k - 1, 8 * v : 8 * v + 8, pair, :] = got[pair]
         copies = []
-        for side in range(SIDES):
+        for side in farthest_first:
             copy = pltpu.make_async_remote_copy(
                 src_ref=send_v.at[k - 1, side + 2],
                 dst_ref=recv_v.at[k - 1, 27 - side],
@@ -280,9 +311,11 @@
             )
             copy.start()
             copies.append(copy)
+        own_values(k)
         return copies
 
-    def rim_forces(k):
+    def rim_contacts(k):
+        work = jnp.zeros((8, 128), F32)
         for v in range(4):
             rows = slice(8 * v, 8 * v + 8)
             a, b = [], []
@@ -297,7 +330,7 @@
                     for c in (2 * pair, 2 * pair + 1):
                         halves = [lanes(recv_q[rows, 2 * c + t, :], far % 128) for t in range(2)]
                         b.append(jnp.where(far >= 128, halves[1], halves[0]))
-            first, _ = response(
+            first, done = response(
                 a, b,
                 [rim_geo[c, rows, :] for c in range(3)],
                 rim_geo[3, rows, :], rim_geo[4, rows, :],
@@ -305,6 +338,10 @@
             )
             for c in range(6):
                 t_rim[pl.ds(64 * v + c, 8, stride=8), :] = first[c]
+            work = work + done
+        return jnp.sum(jnp.where(lane >= 32, work, 0.0), keepdims=True)
+
+    def rim_forces():
         for i in range(SIDES // 2):
             start = 16 * (i + 1)
             even, odd = t_rim[start : start + 8, :], t_rim[start + 8 : start + 16, :]
@@ -369,6 +406,8 @@
             index = jnp.where(ours, seg[0], theirs(0, 0))
             kind = jnp.where(ours, seg[2], theirs(0, 1))
             rim_idx[rows, :] = index.astype(jnp.int32)
+            flipped = jnp.where(ours, theirs(0, 0), seg[0])
+            rim_out[rows, :] = flipped.astype(jnp.int32)
             rim_far[rows, :] = jnp.where(ours, seg[1], theirs(1, 3)).astype(jnp.int32)
             for c in range(3):
                 rim_geo[c, rows, :] = jnp.where(ours, seg[3 + c], -theirs(1, c))
@@ -377,62 +416,97 @@
             coeff = coefficients(kind, valid)
             for q in range(4):
                 rim_geo[5 + q, rows, :] = coeff[q]
-        own_values(0, False)
+        own_values(0)
         turned = jnp.transpose(jnp.concatenate([rim_idx[...].astype(F32), rim_pad], axis=0))
         rim_rows(turned, 0, 0)
 
     sent = list(q_copies)
 
-    def apply(k, copies):
+    def tile(ref, t):
+        return ref[pl.ds(t, 8, stride=8), :]
+
+    def product(k, t, forces):
+        return tile(diag, t) * tile(field.at[k], t) - forces
+
+    def apply(k, copies, finish, between=None):
         whole = local_forces(k)
+        if between is not None:
+            between()
+        for t in range(2, 8):
+            field[k + 1, pl.ds(t, 8, stride=8), :] = finish(product(k, t, whole[:, 128 * t : 128 * (t + 1)]), t)
+        start = [product(k, t, whole[:, 128 * t : 128 * (t + 1)]) for t in range(2)]
         for copy in copies:
             copy.wait_recv()
         if k == 0:
             meet()
-        rim = rim_forces(k)
-        for t in range(8):
-            part = whole[:, 128 * t : 128 * (t + 1)]
-            if t < 2:
-                part = part + rim[:, 128 * t : 128 * (t + 1)]
-            forces[pl.ds(t, 8, stride=8), :] = part
-        return diag * field[k] - forces[0:48, :]
-
-    w0 = field[0]
-    w1 = apply(0, q_copies)
-    field[1] = w1
-    copies = send_values(1)
-    sent += copies
-    early = spread(0, plane, plane_buf.at[0], plane_rank, pack([total_of(w0 * w0), total_of(w0 * w1), total_of(w1 * w1)]))
+        rim_contacts(k)
+        rim = rim_forces()
+        for t in range(2):
+            value = start[t] - rim[:, 128 * t : 128 * (t + 1)]
+            field[k + 1, pl.ds(t, 8, stride=8), :] = finish(value, t)
+        out = send_values(k + 1)
+        sent.extend(out)
+        return out
+
+    def plain(value, t):
+        return value
+
+    def dense_of(k):
+        return field[k, 0:48, :]
+
+    w0 = dense_of(0)
+    copies = apply(0, q_copies, plain)
+    w1 = dense_of(1)
+    first_sums = pack([total_of(w0 * w0), total_of(w0 * w1), total_of(w1 * w1)])
+    early = spread(0, plane, plane_buf.at[0], plane_rank, first_sums)
     sent += early
-    w2 = apply(1, copies)
-    field[2] = w2
-    copies = send_values(2)
-    sent += copies
-    early = spread(1, line, line_buf.at[0], line_rank, gather_sum(early, plane_buf.at[0], PLANE))
-    sent += early
-    w3 = apply(2, copies)
-    early = gather_sum(early, line_buf.at[0], LINE)
-    m0, m1, m2 = lane_of(early, 0), lane_of(early, 1), lane_of(early, 2)
-    inv = jnp.sqrt(m0 / m2)
-    shift = m1 / m0 * inv
-    inv2 = inv * inv
-    u0 = w0
-    w1 = w1 * inv
-    w2 = w2 * inv2
-    w3 = w3 * (inv2 * inv)
-    u1 = w1 - shift * u0
-    u2 = w2 - shift * (2.0 * w1 - shift * u0)
-    u3 = w3 - shift * (3.0 * w2 - shift * (3.0 * w1 - shift * u0))
-    field[3] = u3
-    copies = send_values(3)
-    sent += copies
+    held = {}
+
+    def onward():
+        held["line"] = spread(1, line, line_buf.at[0], line_rank, gather_sum(early, plane_buf.at[0], PLANE))
+        sent.extend(held["line"])
+
+    copies = apply(1, copies, plain, onward)
+
+    def settle():
+        total = gather_sum(held["line"], line_buf.at[0], LINE)
+        m0, m1, m2 = lane_of(total, 0), lane_of(total, 1), lane_of(total, 2)
+        held["inv"] = jnp.sqrt(m0 / m2)
+        held["shift"] = m1 / m0 * held["inv"]
+
+    def centred(value, t):
+        inv, shift = held["inv"], held["shift"]
+        inv2 = inv * inv
+        b, p, q = [tile(field.at[j], t) for j in range(3)]
+        p, q = p * inv, q * inv2
+        return value * (inv2 * inv) - shift * (3.0 * q - shift * (3.0 * p - shift * b))
+
+    copies = apply(2, copies, centred, settle)
+    inv, shift = held["inv"], held["shift"]
+    u0, u3 = w0, dense_of(3)
+    p, q = w1 * inv, dense_of(2) * (inv * inv)
+    u1 = p - shift * u0
+    u2 = q - shift * (2.0 * p - shift * u0)
     basis = [u0, u1, u2, u3]
     pairs = [(0, 0), (0, 1), (1, 1), (1, 2), (2, 2), (2, 3), (3, 3)]
     known = [total_of(basis[i] * basis[j]) for i, j in pairs]
-    u4 = apply(3, copies) * inv - shift * u3
-    last = total_of(u3 * u4)
+    whole = local_forces(3)
+    near_work = jnp.zeros((8, 128), F32)
+    for t in range(8):
+        value = product(3, t, whole[:, 128 * t : 128 * (t + 1)])
+        field[4, pl.ds(t, 8, stride=8), :] = value
+        near_work = near_work + value * tile(field.at[3], t)
+    near_work = inv * jnp.sum(near_work, keepdims=True) - shift * known[6]
+    for copy in copies:
+        copy.wait_recv()
+    last = near_work + inv * rim_contacts(3)
     late = spread(2, plane, plane_buf.at[1], plane_rank, pack(known + [last]))
     sent += late
+    rim = rim_forces()
+    for t in range(2):
+        value = tile(field.at[4], t) - rim[:, 128 * t : 128 * (t + 1)]
+        field[4, pl.ds(t, 8, stride=8), :] = value
+    u4 = dense_of(4) * inv - shift * u3
     late = spread(3, line, line_buf.at[1], line_rank, gather_sum(late, plane_buf.at[1], PLANE))
     sent += late
     sums = gather_sum(late, line_buf.at[1], LINE)
@@ -496,15 +570,23 @@
         x if x.ndim == 2 or x.shape[3] == 2 else x.reshape(x.size // 128, 128) for x in arguments
     ]
     vmem = pl.BlockSpec(memory_space=pltpu.VMEM)
-    smem = pl.BlockSpec(memory_space=pltpu.SMEM)
+    hbm = pl.BlockSpec(memory_space=pltpu.HBM)
     out = jax.ShapeDtypeStruct((48, 128), F32)
     dma = pltpu.SemaphoreType.DMA
     outs = pl.pallas_call(
         kernel,
         out_shape=jax.ShapeDtypeStruct((96,128),F32),
-        in_specs=[vmem, vmem, smem] + [vmem] * 5,
+        in_specs=[hbm] * 8,
         out_specs=vmem,
         scratch_shapes=[
+            pltpu.VMEM((48, 128), F32),
+            pltpu.VMEM((48, 128), F32),
+            pltpu.VMEM((4, 4), F32),
+            pltpu.VMEM((24, 128), jnp.int32),
+            pltpu.VMEM((24, 128), jnp.int32),
+            pltpu.VMEM((24, 128), jnp.int32),
+            pltpu.VMEM((72, 128), F32),
+            pltpu.VMEM((2, 3072), F32),
             pltpu.VMEM((8, 24, 128), F32),
             pltpu.VMEM((24, 128), jnp.int32),
             pltpu.VMEM((24, 128), jnp.int32),
@@ -514,11 +596,12 @@
             pltpu.VMEM((32, 2 * LOCAL_ROWS * 128), BF16),
             pltpu.VMEM((32, 128), jnp.int32),
             pltpu.VMEM((32, 128), jnp.int32),
+            pltpu.VMEM((32, 128), jnp.int32),
             pltpu.VMEM((9, 32, 128), F32),
             pltpu.VMEM((SIDES * 64, RIM), BF16),
             pltpu.VMEM((32 * 8, 128), F32),
             pltpu.VMEM((32, SIDES * 64), BF16),
-            pltpu.VMEM((4, 48, 128), F32),
+            pltpu.VMEM((5, 64, 128), F32),
             pltpu.VMEM((64, 128), F32),
             pltpu.VMEM((3, 32, 128), F32),
             pltpu.VMEM((32, 14, 128), F32),
@@ -528,6 +611,7 @@
             pltpu.VMEM((4, 1, 128), F32),
             pltpu.VMEM((2, PLANE, 1, 128), F32),
             pltpu.VMEM((2, LINE, 1, 128), F32),
+            dma((8,)),
             dma((SIDES,)),
             dma((SIDES,)),
             dma((3, SIDES)),

time: 73.5 us -> 69.6 us (0.947)
  Pallas kernels: 71.2 us -> 67.4 us
    pallas_call x1, Pallas kernels: 71.2 us -> 67.4 us  [shards(): pl.pallas_call(kernel, out_shape=jax.ShapeDtypeStruct((96, 128), F32), in...]
where the time goes in v3:
time: 69.6 us; the launch traced here: 69.4 us
  Pallas kernels  67.4 us (97%)
  local copies, waits for them, and re-layouts  1.38 us (2%)
    pallas_call x1, Pallas kernels, shards(): pl.pallas_call(kernel, out_shape=jax.ShapeDtypeStruct((96, 128), F32), in...  67.4 us

profile of v3, /device:TPU:1, one launch (start us, length us, event | category | flops | bytes accessed | tf_op | source)
XLA Modules:
  0.0 69.4 jit_solution(10743233842111738469)
XLA Ops:
  0.6 67.4 %shard_map.95 = f32[96,128]{1,0:T(8,128)} custom-call(f32[48,128]{1,0:T(8,128)} %bitcast.9, f32[48,128]{1,0:T(8,128)} %bitcast.10, f32[4,4]{1,0:T(4,128)} %stiff_in.1, s32[24,128]{1,0:T(8,128)} %bitcast.13, s32[24,128]{1,0:T(8,128)} %bitcast.14, s32[24,128]{1,0:T(8,128)} %bitcast.15, f32[72,128]{1,0:T(8,128)} %bitcast.8, f32[1,1,1,2,3072]{4,3,2,1,0:T(2,128)} %radii_in.1), custom_call_target="tpu_custom_call" | custom-call | tf_op jit(solution)/shard_map/pallas_call | solution.py:576
  68.0 1.4 %fusion = (f32[48,128]{1,0:T(8,128)}, f32[48,128]{1,0:T(8,128)}) fusion(f32[96,128]{1,0:T(8,128)} %shard_map.95), kind=kLoop, calls=%fused_computation | loop fusion | bytes 98304 | tf_op jit(solution)/shard_map/slice | solution.py:626

commit v4 on v3

--- a/solution.py
+++ b/solution.py
@@ -575,7 +575,7 @@
     dma = pltpu.SemaphoreType.DMA
     outs = pl.pallas_call(
         kernel,
-        out_shape=jax.ShapeDtypeStruct((96,128),F32),
+        out_shape=pltpu.VMEM((96, 128), F32),
         in_specs=[hbm] * 8,
         out_specs=vmem,
         scratch_shapes=[

time: 69.6 us -> 68.2 us (0.980)
  local copies, waits for them, and re-layouts: 1.38 us -> 0.62 us
    slice x1, local copies, waits for them, and re-layouts: 1.38 us -> 0.62 us  [shards(): outs[48 * i:48 * i + 48].reshape(1, 1, 1, 6, GRAINS)]
where the time goes in v4:
time: 68.2 us; the launch traced here: 68 us
  Pallas kernels  66.8 us (98%)
    pallas_call x1, Pallas kernels, shards(): pl.pallas_call(kernel, out_shape=pltpu.VMEM((96, 128), F32), in_specs=[hb...  66.8 us

profile of v4, /device:TPU:1, one launch (start us, length us, event | category | flops | bytes accessed | tf_op | source)
XLA Modules:
  0.0 68.0 jit_solution(14901994779634060403)
XLA Ops:
  0.6 66.8 %shard_map.95 = f32[96,128]{1,0:T(8,128)S(1)} custom-call(f32[48,128]{1,0:T(8,128)} %bitcast.9, f32[48,128]{1,0:T(8,128)} %bitcast.10, f32[4,4]{1,0:T(4,128)} %stiff_in.1, s32[24,128]{1,0:T(8,128)} %bitcast.13, s32[24,128]{1,0:T(8,128)} %bitcast.14, s32[24,128]{1,0:T(8,128)} %bitcast.15, f32[72,128]{1,0:T(8,128)} %bitcast.8, f32[1,1,1,2,3072]{4,3,2,1,0:T(2,128)} %radii_in.1), custom_call_target="tpu_custom_call" | custom-call | tf_op jit(solution)/shard_map/pallas_call | solution.py:576
  67.4 0.6 fusion

commit v5 on v4

--- a/solution.py
+++ b/solution.py
@@ -174,18 +174,26 @@
 
     pl.semaphore_wait(barrier, SIDES + PLANE - 1 + LINE - 1)
 
-    q_copies = []
-    for side in farthest_first:
-        copy = pltpu.make_async_remote_copy(
-            src_ref=send_q.at[side + 2],
-            dst_ref=recv_q.at[27 - side],
-            send_sem=q_send.at[side],
-            recv_sem=q_recv.at[25 - side],
-            device_id=near[side],
+    def exchange(source, target, send_sem, recv_sem):
+        for side in farthest_first:
+            pltpu.make_async_remote_copy(
+                src_ref=source.at[side + 2],
+                dst_ref=target.at[27 - side],
+                send_sem=send_sem,
+                recv_sem=recv_sem,
+                device_id=near[side],
+                device_id_type=MESH,
+            ).start()
+        return pltpu.make_async_remote_copy(
+            src_ref=source.at[2:28],
+            dst_ref=target.at[2:28],
+            send_sem=send_sem,
+            recv_sem=recv_sem,
+            device_id=near[0],
             device_id_type=MESH,
         )
-        copy.start()
-        q_copies.append(copy)
+
+    arriving = exchange(send_q, recv_q, q_send.at[0], q_recv.at[0])
 
     for v in range(3):
         rows = slice(8 * v, 8 * v + 8)
@@ -299,20 +307,9 @@
             got = rim_values(k, rim_out, v)
             for pair in range(3):
                 send_v[k - 1, 8 * v : 8 * v + 8, pair, :] = got[pair]
-        copies = []
-        for side in farthest_first:
-            copy = pltpu.make_async_remote_copy(
-                src_ref=send_v.at[k - 1, side + 2],
-                dst_ref=recv_v.at[k - 1, 27 - side],
-                send_sem=v_send.at[k - 1, side],
-                recv_sem=v_recv.at[k - 1, 25 - side],
-                device_id=near[side],
-                device_id_type=MESH,
-            )
-            copy.start()
-            copies.append(copy)
+        out = exchange(send_v.at[k - 1], recv_v.at[k - 1], v_send.at[k - 1], v_recv.at[k - 1])
         own_values(k)
-        return copies
+        return out
 
     def rim_contacts(k):
         work = jnp.zeros((8, 128), F32)
@@ -367,23 +364,27 @@
     def spread(stage, where, buffer, rank, value):
         row_buf[stage] = value
         buffer[rank] = value
-        copies = []
-        for j, device in enumerate(where):
-            copy = pltpu.make_async_remote_copy(
+        for device in where:
+            pltpu.make_async_remote_copy(
                 src_ref=row_buf.at[stage],
                 dst_ref=buffer.at[rank],
-                send_sem=s_send.at[stage, j],
-                recv_sem=s_recv.at[stage, j],
+                send_sem=s_send.at[stage],
+                recv_sem=s_recv.at[stage],
                 device_id=device,
                 device_id_type=MESH,
-            )
-            copy.start()
-            copies.append(copy)
-        return copies
-
-    def gather_sum(copies, buffer, count):
-        for copy in copies:
-            copy.wait_recv()
+            ).start()
+        count = len(where)
+        return pltpu.make_async_remote_copy(
+            src_ref=buffer.at[0:count],
+            dst_ref=buffer.at[0:count],
+            send_sem=s_send.at[stage],
+            recv_sem=s_recv.at[stage],
+            device_id=where[0],
+            device_id_type=MESH,
+        )
+
+    def gather_sum(arriving, buffer, count):
+        arriving.wait_recv()
         level = [buffer[j] for j in range(count)]
         while len(level) > 1:
             level = [level[j] + level[j + 1] for j in range(0, len(level), 2)]
@@ -420,7 +421,7 @@
         turned = jnp.transpose(jnp.concatenate([rim_idx[...].astype(F32), rim_pad], axis=0))
         rim_rows(turned, 0, 0)
 
-    sent = list(q_copies)
+    sent = [arriving]
 
     def tile(ref, t):
         return ref[pl.ds(t, 8, stride=8), :]
@@ -428,15 +429,14 @@
     def product(k, t, forces):
         return tile(diag, t) * tile(field.at[k], t) - forces
 
-    def apply(k, copies, finish, between=None):
+    def apply(k, arriving, finish, between=None):
         whole = local_forces(k)
         if between is not None:
             between()
         for t in range(2, 8):
             field[k + 1, pl.ds(t, 8, stride=8), :] = finish(product(k, t, whole[:, 128 * t : 128 * (t + 1)]), t)
         start = [product(k, t, whole[:, 128 * t : 128 * (t + 1)]) for t in range(2)]
-        for copy in copies:
-            copy.wait_recv()
+        arriving.wait_recv()
         if k == 0:
             meet()
         rim_contacts(k)
@@ -445,7 +445,7 @@
             value = start[t] - rim[:, 128 * t : 128 * (t + 1)]
             field[k + 1, pl.ds(t, 8, stride=8), :] = finish(value, t)
         out = send_values(k + 1)
-        sent.extend(out)
+        sent.append(out)
         return out
 
     def plain(value, t):
@@ -455,18 +455,18 @@
         return field[k, 0:48, :]
 
     w0 = dense_of(0)
-    copies = apply(0, q_copies, plain)
+    arriving = apply(0, arriving, plain)
     w1 = dense_of(1)
     first_sums = pack([total_of(w0 * w0), total_of(w0 * w1), total_of(w1 * w1)])
     early = spread(0, plane, plane_buf.at[0], plane_rank, first_sums)
-    sent += early
+    sent.append(early)
     held = {}
 
     def onward():
         held["line"] = spread(1, line, line_buf.at[0], line_rank, gather_sum(early, plane_buf.at[0], PLANE))
-        sent.extend(held["line"])
-
-    copies = apply(1, copies, plain, onward)
+        sent.append(held["line"])
+
+    arriving = apply(1, arriving, plain, onward)
 
     def settle():
         total = gather_sum(held["line"], line_buf.at[0], LINE)
@@ -481,7 +481,7 @@
         p, q = p * inv, q * inv2
         return value * (inv2 * inv) - shift * (3.0 * q - shift * (3.0 * p - shift * b))
 
-    copies = apply(2, copies, centred, settle)
+    arriving = apply(2, arriving, centred, settle)
     inv, shift = held["inv"], held["shift"]
     u0, u3 = w0, dense_of(3)
     p, q = w1 * inv, dense_of(2) * (inv * inv)
@@ -497,19 +497,21 @@
         field[4, pl.ds(t, 8, stride=8), :] = value
         near_work = near_work + value * tile(field.at[3], t)
     near_work = inv * jnp.sum(near_work, keepdims=True) - shift * known[6]
-    for copy in copies:
-        copy.wait_recv()
+    arriving.wait_recv()
     last = near_work + inv * rim_contacts(3)
     late = spread(2, plane, plane_buf.at[1], plane_rank, pack(known + [last]))
-    sent += late
     rim = rim_forces()
     for t in range(2):
         value = tile(field.at[4], t) - rim[:, 128 * t : 128 * (t + 1)]
         field[4, pl.ds(t, 8, stride=8), :] = value
     u4 = dense_of(4) * inv - shift * u3
-    late = spread(3, line, line_buf.at[1], line_rank, gather_sum(late, plane_buf.at[1], PLANE))
-    sent += late
+    for done in sent:
+        done.wait_send()
+    sums = gather_sum(late, plane_buf.at[1], PLANE)
+    late.wait_send()
+    late = spread(3, line, line_buf.at[1], line_rank, sums)
     sums = gather_sum(late, line_buf.at[1], LINE)
+    late.wait_send()
     mu = [lane_of(sums, j) for j in range(8)]
 
     scale = 1.0 / inv
@@ -561,8 +563,6 @@
         r = r + res[i] * basis[i]
     x_ref[0:48] = x
     x_ref[48:96] = r
-    for copy in sent:
-        copy.wait_send()
 
 
 def shards(*arguments):
@@ -612,12 +612,12 @@
             pltpu.VMEM((2, PLANE, 1, 128), F32),
             pltpu.VMEM((2, LINE, 1, 128), F32),
             dma((8,)),
-            dma((SIDES,)),
-            dma((SIDES,)),
-            dma((3, SIDES)),
-            dma((3, SIDES)),
-            dma((4, PLANE)),
-            dma((4, PLANE)),
+            dma((1,)),
+            dma((1,)),
+            dma((3,)),
+            dma((3,)),
+            dma((4,)),
+            dma((4,)),
         ],
         compiler_params=pltpu.CompilerParams(
             collective_id=0, has_side_effects=True, vmem_limit_bytes=56 * 1024 * 1024

time: 68.2 us -> 63.8 us (0.935)
  Pallas kernels: 66.8 us -> 62.3 us
    pallas_call x1, Pallas kernels: 66.8 us -> 62.3 us  [shards(): pl.pallas_call(kernel, out_shape=pltpu.VMEM((96, 128), F32), in_specs=[hb...]
where the time goes in v5:
time: 63.8 us; the launch traced here: 63.6 us
  Pallas kernels  62.3 us (98%)
  between operations  0.64 us (1%)
    pallas_call x1, Pallas kernels, shards(): pl.pallas_call(kernel, out_shape=pltpu.VMEM((96, 128), F32), in_specs=[hb...  62.3 us

profile of v5, /device:TPU:1, one launch (start us, length us, event | category | flops | bytes accessed | tf_op | source)
XLA Modules:
  0.0 63.6 jit_solution(1330696232960324305)
XLA Ops:
  0.6 62.3 %shard_map.95 = f32[96,128]{1,0:T(8,128)S(1)} custom-call(f32[48,128]{1,0:T(8,128)} %bitcast.9, f32[48,128]{1,0:T(8,128)} %bitcast.10, f32[4,4]{1,0:T(4,128)} %stiff_in.1, s32[24,128]{1,0:T(8,128)} %bitcast.13, s32[24,128]{1,0:T(8,128)} %bitcast.14, s32[24,128]{1,0:T(8,128)} %bitcast.15, f32[72,128]{1,0:T(8,128)} %bitcast.8, f32[1,1,1,2,3072]{4,3,2,1,0:T(2,128)} %radii_in.1), custom_call_target="tpu_custom_call" | custom-call | tf_op jit(solution)/shard_map/pallas_call | solution.py:576
  62.9 0.6 fusion

commit v6 on v5

--- a/solution.py
+++ b/solution.py
@@ -69,7 +69,7 @@
     dense, idx_a, idx_b, geo, one_hot, t_local, lhs_local,
     rim_idx, rim_far, rim_out, rim_geo, rim_hot, t_rim, lhs_rim, field, diag, mine,
     send_q, recv_q, send_v, recv_v, row_buf, plane_buf, line_buf,
-    in_sem, q_send, q_recv, v_send, v_recv, s_send, s_recv,
+    out_sem, q_recv, v_recv, s_recv,
 ):
     loads = []
     for j, (source, target) in enumerate((
@@ -77,7 +77,7 @@
         (normal_in, normal_ref), (radii_in.at[0, 0, 0], radii_ref), (stiff_in, stiff_ref),
         (diag_in, diag_ref),
     )):
-        load = pltpu.make_async_copy(source, target, in_sem.at[j])
+        load = pltpu.make_async_copy(source, target, out_sem.at[j])
         load.start()
         loads.append(load)
     gx, gy, gz = lax.axis_index("gx"), lax.axis_index("gy"), lax.axis_index("gz")
@@ -107,7 +107,7 @@
     row = lax.broadcasted_iota(jnp.int32, (8, 128), 0)
 
     barrier = pltpu.get_barrier_semaphore()
-    for where in near + plane + line:
+    for where in [near[side] for side in farthest_first] + line + plane:
         pl.semaphore_signal(barrier, inc=1, device_id=where, device_id_type=MESH)
 
     recv_q[0:2] = jnp.zeros((2, 14, 128), F32)
@@ -193,7 +193,7 @@
             device_id_type=MESH,
         )
 
-    arriving = exchange(send_q, recv_q, q_send.at[0], q_recv.at[0])
+    arriving = exchange(send_q, recv_q, out_sem.at[0], q_recv.at[0])
 
     for v in range(3):
         rows = slice(8 * v, 8 * v + 8)
@@ -307,7 +307,7 @@
             got = rim_values(k, rim_out, v)
             for pair in range(3):
                 send_v[k - 1, 8 * v : 8 * v + 8, pair, :] = got[pair]
-        out = exchange(send_v.at[k - 1], recv_v.at[k - 1], v_send.at[k - 1], v_recv.at[k - 1])
+        out = exchange(send_v.at[k - 1], recv_v.at[k - 1], out_sem.at[k], v_recv.at[k - 1])
         own_values(k)
         return out
 
@@ -368,7 +368,7 @@
             pltpu.make_async_remote_copy(
                 src_ref=row_buf.at[stage],
                 dst_ref=buffer.at[rank],
-                send_sem=s_send.at[stage],
+                send_sem=out_sem.at[4 + stage],
                 recv_sem=s_recv.at[stage],
                 device_id=device,
                 device_id_type=MESH,
@@ -377,7 +377,7 @@
         return pltpu.make_async_remote_copy(
             src_ref=buffer.at[0:count],
             dst_ref=buffer.at[0:count],
-            send_sem=s_send.at[stage],
+            send_sem=out_sem.at[4 + stage],
             recv_sem=s_recv.at[stage],
             device_id=where[0],
             device_id_type=MESH,
@@ -613,10 +613,7 @@
             pltpu.VMEM((2, LINE, 1, 128), F32),
             dma((8,)),
             dma((1,)),
-            dma((1,)),
             dma((3,)),
-            dma((3,)),
-            dma((4,)),
             dma((4,)),
         ],
         compiler_params=pltpu.CompilerParams(

time: 63.8 us -> 63.6 us (level)
  no operation moved by 1% of the time
where the time goes in v6:
time: 63.6 us; the launch traced here: 63.4 us
  Pallas kernels  62.1 us (98%)
  between operations  0.64 us (1%)
    pallas_call x1, Pallas kernels, shards(): pl.pallas_call(kernel, out_shape=pltpu.VMEM((96, 128), F32), in_specs=[hb...  62.1 us

profile of v6, /device:TPU:1, one launch (start us, length us, event | category | flops | bytes accessed | tf_op | source)
XLA Modules:
  0.0 63.4 jit_solution(6844281810077433365)
XLA Ops:
  0.6 62.1 %shard_map.95 = f32[96,128]{1,0:T(8,128)S(1)} custom-call(f32[48,128]{1,0:T(8,128)} %bitcast.9, f32[48,128]{1,0:T(8,128)} %bitcast.10, f32[4,4]{1,0:T(4,128)} %stiff_in.1, s32[24,128]{1,0:T(8,128)} %bitcast.13, s32[24,128]{1,0:T(8,128)} %bitcast.14, s32[24,128]{1,0:T(8,128)} %bitcast.15, f32[72,128]{1,0:T(8,128)} %bitcast.8, f32[1,1,1,2,3072]{4,3,2,1,0:T(2,128)} %radii_in.1), custom_call_target="tpu_custom_call" | custom-call | tf_op jit(solution)/shard_map/pallas_call | solution.py:576
  62.8 0.6 fusion
